TPU v7x, 256 devices: a whole 4x4x8 slice. The times are simulated.
256 devices in a mesh: gx: 64 (over y, x_lo, z), gy: 4 (over x_hi, core).
Axes of the slice: x: 4 (x_hi: 2, x_lo: 2; x = x_hi * 2 + x_lo), y: 4, z: 8, core: 2. Of those that a mesh axis runs over, the one named last changes fastest.
Arguments:
- positions: float32 [3, 128, 8, 256], P(None, 'gx', 'gy'), may hold values from 0 to 16, as said below
- velocities: float32 [3, 128, 8, 256], P(None, 'gx', 'gy'), may hold values from -3 to 3
- occupancy: int32 [128, 8], P('gx', 'gy'), may hold values from 64 to 256
- cot_positions: float32 [3, 128, 8, 256], P(None, 'gx', 'gy'), may hold values from -6 to 6
- cot_velocities: float32 [3, 128, 8, 256], P(None, 'gx', 'gy'), may hold values from -6 to 6
Outputs:
- grad_positions: float32 [3, 128, 8, 256], P(None, 'gx', 'gy')
- grad_velocities: float32 [3, 128, 8, 256], P(None, 'gx', 'gy')
Inputs may be any that keep to these rules, and one draw needn't show every extreme that they name: `positions`: components 0 and 1 lie in [0, 1), the offset in the tile's cell; component 2 lies in [0, 16). Slots 0 to occupancy - 1 of a tile hold particles, the other slots are empty.
All inputs are finite; a program needn't handle non-finite values.
Results may differ from a plain program's by a relative error of at most 0.0003.
Values sent between devices are 32-bit elements; how exact they have to be, the bound alone decides.
A program may use at most 128 MiB of HBM per device.

v0:
```python
import functools

import jax
import jax.numpy as jnp
from jax import lax
from jax.experimental import pallas as pl
from jax.experimental.pallas import tpu as pltpu
from jax.sharding import PartitionSpec as P

STEPS = 4
DT = 0.05
MU = 0.15
MESH = pl.DeviceIdType.MESH
F32 = jnp.float32
I32 = jnp.int32
NJ, NI = 32, 8
SB = 32
NS = 128
REACH = 1.0001


def logical_to_mesh(gx, gy):
    pair = gx // 32
    s = gx + pair * (63 - 2 * gx)
    y = s // 8
    zz = s % 8
    z = zz + (y % 2) * (7 - 2 * zz)
    core = (gy * (3 - gy)) // 2
    x = pair * 3 + (gy // 2) * (1 - 2 * pair)
    return (y * 2 + x % 2) * 8 + z, (x // 2) * 2 + core


def mesh_to_logical(gx, gy):
    y = gx // 16
    xl = (gx // 8) % 2
    z = gx % 8
    pair = gy // 2
    core = gy % 2
    s = 8 * y + z + (y % 2) * (7 - 2 * z)
    return s + pair * (63 - 2 * s), core + (xl + pair * (1 - 2 * xl)) * (3 - 2 * core)


def halo_kernel(nx, ny, src, out, send_sem, recv_sem):
    gx, gy = mesh_to_logical(lax.axis_index("gx"), lax.axis_index("gy"))
    xm, xp = (gx + nx - 1) % nx, (gx + 1) % nx
    up, down = gy + 1 < ny, gy > 0
    barrier = pltpu.get_barrier_semaphore()

    def greet(x, y):
        pl.semaphore_signal(barrier, inc=1, device_id=logical_to_mesh(x, y), device_id_type=MESH)

    @pl.when(down)
    def _():
        for x in (xm, xp, gx):
            greet(x, gy - 1)

    @pl.when(up)
    def _():
        for x in (xm, xp, gx):
            greet(x, gy + 1)

    greet(xm, gy)
    greet(xp, gy)
    peers = 2 + 3 * (1 - gy // (ny - 1)) + 3 * ((gy + ny - 2) // (ny - 1))
    pl.semaphore_wait(barrier, peers)

    def go(k, start, dest, n, x, y, what):
        copy = pltpu.make_async_remote_copy(
            src_ref=src.at[:, pl.ds(start, n)],
            dst_ref=out.at[:, pl.ds(dest, n)],
            send_sem=send_sem.at[k],
            recv_sem=recv_sem.at[k],
            device_id=logical_to_mesh(x, y),
            device_id_type=MESH,
        )
        getattr(copy, what)()

    def along(what):
        go(0, 512, 0, 512, xp, gy, what)
        go(1, 0, 512, 512, xm, gy, what)

    def upward(what):
        go(4, 768, 2048, 256, xp, gy + 1, what)
        go(5, 256, 2304, 256, xm, gy + 1, what)
        go(2, 256, 1024, 256, gx, gy + 1, what)
        go(3, 768, 1280, 256, gx, gy + 1, what)

    def downward(what):
        go(8, 512, 2560, 256, xp, gy - 1, what)
        go(9, 0, 2816, 256, xm, gy - 1, what)
        go(6, 0, 1536, 256, gx, gy - 1, what)
        go(7, 512, 1792, 256, gx, gy - 1, what)

    @pl.when(up)
    def _():
        upward("start")

    @pl.when(down)
    def _():
        downward("start")

    along("start")
    along("wait")

    @pl.when(up)
    def _():
        upward("wait_send")
        downward("wait_recv")

    @pl.when(down)
    def _():
        downward("wait_send")
        upward("wait_recv")


VM = pl.BlockSpec(memory_space=pltpu.VMEM)
SM = pl.BlockSpec(memory_space=pltpu.SMEM)


def halo(own, nx, ny, cid):
    rows = own.shape[0]
    return pl.pallas_call(
        functools.partial(halo_kernel, nx, ny),
        out_shape=jax.ShapeDtypeStruct((rows, 3072), F32),
        in_specs=[VM],
        out_specs=VM,
        scratch_shapes=[pltpu.SemaphoreType.DMA((10,)), pltpu.SemaphoreType.DMA((10,))],
        compiler_params=pltpu.CompilerParams(
            collective_id=cid, has_side_effects=True, vmem_limit_bytes=2 << 20
        ),
        name=f"halo{rows}",
    )(own)


def iota(shape, dim):
    return lax.broadcasted_iota(I32, shape, dim)


def dot_t(a, b):
    return lax.dot_general(a, b, (((1,), (1,)), ((), ())), preferred_element_type=F32)


def plan_kernel(own, hal, ok, tab_j, tab_i, cnt, pre):
    sub = iota((NS, 128), 0)
    lane = iota((NS, 128), 1)
    upper = jnp.where(sub <= lane, 1.0, 0.0).astype(jnp.bfloat16)
    strict = jnp.where(lane < sub, 1.0, 0.0)

    def row(k):
        if k < NI:
            z = own[2:3, 128 * k : 128 * k + 128]
            live = own[6:7, 128 * k : 128 * k + 128] > 0.5
        else:
            s = 128 * (k - NI)
            good = ok[0:1, s : s + 128] > 0.5
            z = jnp.where(good, hal[2:3, s : s + 128], 0.0)
            live = jnp.where(good, hal[6:7, s : s + 128], 0.0) > 0.5
        bucket = jnp.clip((z * 8.0).astype(I32), 0, NS - 1)
        return jnp.where(live, bucket, -1)

    carry = jnp.zeros((NS, 1), F32)
    total_i = carry
    for k in range(NJ):
        hot = jnp.where(sub == row(k), 1.0, 0.0)
        count = jnp.dot(hot.astype(jnp.bfloat16), upper, preferred_element_type=F32)
        pre[:, 128 * k : 128 * k + 128] = count + carry - 1.0
        carry = carry + count[:, 127:128]
        if k == NI - 1:
            total_i = carry
    hi = lax.Precision.HIGHEST
    off_j = jnp.dot(strict, jnp.broadcast_to(carry, (NS, 128)), precision=hi, preferred_element_type=F32)
    off_i = jnp.dot(strict, jnp.broadcast_to(total_i, (NS, 128)), precision=hi, preferred_element_type=F32)

    def inverse(blocks, offset, nh, k, acc):
        b = row(k)
        rank = jnp.sum(
            jnp.where(sub == b, pre[:, 128 * k : 128 * k + 128] + offset, 0.0), axis=0, keepdims=True
        ).astype(I32)
        rank = jnp.where(b >= 0, rank, -128)
        high, low = rank >> 7, rank & 127
        eq = iota((nh, 128), 0) == high
        a = jnp.concatenate(
            [jnp.where(eq, iota((nh, 128), 1), 0), jnp.where(eq, k + 1, 0)], axis=0
        ).astype(F32).astype(jnp.bfloat16)
        hot = jnp.where(sub == low, 1.0, 0.0).astype(jnp.bfloat16)
        return acc + dot_t(a, hot), high, low

    acc = jnp.zeros((2 * NJ, 128), F32)
    for k in range(NJ):
        acc, _, _ = inverse(NJ, off_j, NJ, k, acc)
    tab_j[0:NJ, :] = acc[0:NJ].astype(I32)
    tab_j[NJ : 2 * NJ, :] = acc[NJ:].astype(I32) - 1
    acc = jnp.zeros((2 * NI, 128), F32)
    for k in range(NI):
        acc, high, low = inverse(NI, off_i, NI, k, acc)
        tab_i[16 + k : 17 + k, :] = high
        tab_i[24 + k : 25 + k, :] = jnp.maximum(low, 0)
    tab_i[0:NI, :] = acc[0:NI].astype(I32)
    tab_i[NI : 2 * NI, :] = acc[NI:].astype(I32) - 1
    nj = jnp.sum(carry, axis=0, keepdims=True)
    ni = jnp.sum(total_i, axis=0, keepdims=True)
    at = iota((1, 128), 1)
    blocks_j = (nj + 127.0).astype(I32) >> 7
    groups_i = (ni + (SB - 1.0)).astype(I32) >> 5
    cnt[...] = jnp.where(at == 0, blocks_j, groups_i)


def plan(own, hal, ok):
    return pl.pallas_call(
        plan_kernel,
        out_shape=(
            jax.ShapeDtypeStruct((2 * NJ, 128), I32),
            jax.ShapeDtypeStruct((32, 128), I32),
            jax.ShapeDtypeStruct((1, 128), I32),
        ),
        in_specs=[VM] * 3,
        out_specs=(VM, VM, VM),
        scratch_shapes=[pltpu.VMEM((NS, 4096), F32)],
        compiler_params=pltpu.CompilerParams(vmem_limit_bytes=8 << 20),
        name="plan",
    )(own, hal, ok)


def take(block, idx):
    return jnp.take_along_axis(block, idx, axis=1, mode="promise_in_bounds")


def gather(load, count, table, lane_row, blk_row):
    idx = jnp.broadcast_to(table[pl.ds(lane_row, 1), :], (8, 128))
    blk = jnp.broadcast_to(table[pl.ds(blk_row, 1), :], (8, 128))
    out = jnp.zeros((8, 128), F32)
    for k in range(count):
        out = jnp.where(blk == k, take(load(k), idx), out)
    return out


def source(own, hal, extra=None):
    def load(k):
        part = own[0:8, 128 * k : 128 * k + 128] if k < NI else hal[0:8, 128 * (k - NI) : 128 * (k - NI) + 128]
        if extra is not None:
            part = jnp.where(iota((8, 128), 0) < 6, part, 0.0) + extra[:, 128 * k : 128 * k + 128]
        return part

    return load


def block(ref, m):
    return ref[:, pl.ds(pl.multiple_of(m * 128, 128), 128)]


def put(ref, m, value):
    ref[:, pl.ds(pl.multiple_of(m * 128, 128), 128)] = value


def columns(ref, k, rows):
    ref[128 * k : 128 * k + 128, :] = rows.T


def columns_to_own(cols, rows, tab_i, store):
    for k in range(NI):
        rows[:, 128 * k : 128 * k + 128] = cols[128 * k : 128 * k + 128, :].T
    load = lambda m: rows[:, 128 * m : 128 * m + 128]
    for k in range(NI):
        store(k, gather(load, NI, tab_i, 24 + k, 16 + k))


def pairs(cnt, win, body, channels, cols, n_out):
    def group(g, _):
        at = pl.multiple_of(g * SB, SB)
        picked = [
            jnp.broadcast_to(ref[pl.ds(at, SB), c : c + 1], (SB, 128)) for ref, c in channels
        ]
        first = win[g >> 2, g & 3]
        last = win[g >> 2, (g & 3) + 4]
        sums = lax.fori_loop(
            first,
            last,
            lambda m, acc: body(m, picked, acc),
            tuple(jnp.zeros((SB, 128), F32) for _ in range(n_out)),
        )
        for c, total in enumerate(sums):
            cols[pl.ds(at, SB), c : c + 1] = jnp.sum(total, axis=1, keepdims=True)
        return 0

    lax.fori_loop(0, cnt[0, 1], group, 0)


def row_of(ref, c, m):
    return jnp.broadcast_to(ref[c : c + 1, pl.ds(pl.multiple_of(m * 128, 128), 128)], (SB, 128))


def geometry(mj, mr, m, xi, yi, zi, sx, sy):
    dx = row_of(mj, 0, m) - xi
    dy = row_of(mj, 1, m) - yi
    dz = row_of(mj, 2, m) - zi
    top = jnp.broadcast_to(mr[pl.ds(m, 1), :], (SB, 128)) - sx * row_of(mj, 6, m) - sy * row_of(mj, 7, m)
    q = jnp.maximum(top - (dx * dx + dy * dy + dz * dz), 0.0)
    return dx, dy, dz, q


GEO = (0, 1, 2, 6, 7)


def live_of(tab_i, k):
    return jnp.broadcast_to(tab_i[16 + k : 17 + k, :], (8, 128)) >= 0


def density_kernel(cnt, own, hal, attr_j, attr_i, tab_j, tab_i, mj, mr, ic, win, rho, cols, rows, zlo, zhi, win_s, sem):
    load = source(own, hal, attr_j)
    zlo[...] = jnp.full((NJ, 128), 1e30, F32)
    zhi[...] = jnp.full((NJ, 128), -1e30, F32)

    def fill(m, _):
        got = gather(load, NJ, tab_j, m, NJ + m)
        put(mj, m, got)
        held = tab_j[pl.ds(NJ + m, 1), :] >= 0
        mr[pl.ds(m, 1), :] = jnp.where(held, 1.0 - jnp.abs(got[6:7]) - jnp.abs(got[7:8]), -1.0)
        zlo[pl.ds(m, 1), :] = jnp.where(held, got[2:3], 1e30)
        zhi[pl.ds(m, 1), :] = jnp.where(held, got[2:3], -1e30)
        return 0

    lax.fori_loop(0, cnt[0, 0], fill, 0)
    load_i = source(own, hal, attr_i)
    z_rows = []
    for k in range(NI):
        got = gather(load_i, NI, tab_i, k, NI + k)
        columns(ic, k, got)
        z_rows.append(got[2:3])
    z_i = jnp.concatenate(z_rows, axis=0)
    held_i = tab_i[NI : 2 * NI, :] >= 0
    eye = iota((NJ, 128), 0) == iota((NJ, 128), 1)
    low_j = jnp.sum(jnp.where(eye, jnp.min(zlo[...], axis=1, keepdims=True), 0.0), axis=0, keepdims=True)
    high_j = jnp.sum(jnp.where(eye, jnp.max(zhi[...], axis=1, keepdims=True), 0.0), axis=0, keepdims=True)
    lane = iota((NI, 128), 1)
    windows = jnp.zeros((NI, 128), I32)
    lane_f = lane.astype(F32)
    for g in range(4):
        inside = held_i & (lane >= SB * g) & (lane < SB * g + SB)
        low = jnp.min(jnp.where(inside, z_i, 1e30), axis=1, keepdims=True)
        high = jnp.max(jnp.where(inside, z_i, -1e30), axis=1, keepdims=True)
        meets = (high_j > low - REACH) & (low_j < high + REACH) & (lane < NJ)
        first = jnp.min(jnp.where(meets, lane_f, 99.0), axis=1, keepdims=True).astype(I32)
        last = jnp.max(jnp.where(meets, lane_f + 1.0, 0.0), axis=1, keepdims=True).astype(I32)
        windows = jnp.where(lane == g, first, windows)
        windows = jnp.where(lane == g + 4, last, windows)
    win[...] = windows
    copy = pltpu.make_async_copy(win, win_s, sem)
    copy.start()
    copy.wait()

    def body(m, picked, acc):
        _, _, _, q = geometry(mj, mr, m, *picked)
        return (acc[0] + q * q * q,)

    pairs(cnt, win_s, body, [(ic, c) for c in GEO], cols, 1)

    def store(k, got):
        rho[:, 128 * k : 128 * k + 128] = MU * got

    columns_to_own(cols, rows, tab_i, store)


def call(kernel, name, ins, smem, outs, scratch=()):
    specs = [SM if i in smem else VM for i in range(len(ins))]
    return pl.pallas_call(
        kernel,
        out_shape=tuple(jax.ShapeDtypeStruct(s, t) for s, t in outs),
        in_specs=specs,
        out_specs=tuple(VM for _ in outs),
        scratch_shapes=list(scratch),
        compiler_params=pltpu.CompilerParams(vmem_limit_bytes=8 << 20),
        name=name,
    )(*ins)


COLS = ((1024, 8), F32)
OWN = ((8, 1024), F32)
WIDE = ((8, 4096), F32)


def density(cnt, own, hal, attr_j, attr_i, tab_j, tab_i):
    return call(
        density_kernel,
        "density",
        (cnt, own, hal, attr_j, attr_i, tab_j, tab_i),
        (0,),
        (WIDE, ((NJ, 128), F32), COLS, ((NI, 128), I32), OWN),
        (
            pltpu.VMEM((1024, 8), F32),
            pltpu.VMEM((8, 1024), F32),
            pltpu.VMEM((NJ, 128), F32),
            pltpu.VMEM((NJ, 128), F32),
            pltpu.SMEM((NI, 128), I32),
            pltpu.SemaphoreType.DMA,
        ),
    )


def pressure(rho_row, held):
    padded = jnp.where(held, rho_row, 1.0)
    inverse = 1.0 / padded
    return 24.0 * (padded - 1.0) * inverse * inverse, 3.0 * inverse


def pressure_tables(cnt, rho, rho_h, tab_j, tab_i, mc, cc):
    load = source(rho, rho_h)
    row8 = iota((8, 128), 0)

    def table(got, held):
        coef, inv = pressure(got[0:1], held)
        return jnp.where(row8 == 0, coef, jnp.where(row8 == 1, inv, 0.0))

    def fill(m, _):
        put(mc, m, table(gather(load, NJ, tab_j, m, NJ + m), tab_j[pl.ds(NJ + m, 1), :] >= 0))
        return 0

    lax.fori_loop(0, cnt[0, 0], fill, 0)
    for k in range(NI):
        columns(cc, k, table(gather(load, NI, tab_i, k, NI + k), tab_i[NI + k : NI + k + 1, :] >= 0))


def force_kernel(cnt, win, rho, rho_h, own, mj, mr, ic, tab_j, tab_i, mc, cc, new, cols, rows):
    pressure_tables(cnt, rho, rho_h, tab_j, tab_i, mc, cc)

    def body(m, picked, acc):
        xi, yi, zi, sx, sy, ux, uy, uz, ci = picked
        dx, dy, dz, q = geometry(mj, mr, m, xi, yi, zi, sx, sy)
        q2 = q * q
        push = (ci + row_of(mc, 0, m)) * q2
        drag = q2 * q * row_of(mc, 1, m) * (1.0 / 6.0)
        return (
            acc[0] + (drag * (row_of(mj, 3, m) - ux) - push * dx),
            acc[1] + (drag * (row_of(mj, 4, m) - uy) - push * dy),
            acc[2] + (drag * (row_of(mj, 5, m) - uz) - push * dz),
        )

    pairs(cnt, win, body, [(ic, c) for c in GEO + (3, 4, 5)] + [(cc, 0)], cols, 3)
    row8 = iota((8, 128), 0)

    def store(k, got):
        at = slice(128 * k, 128 * k + 128)
        v = [own[3 + c : 4 + c, at] + (DT * MU) * got[c : c + 1] for c in range(3)]
        x = [own[c : c + 1, at] + DT * v[c] for c in range(3)]
        new[0:3, at] = jnp.concatenate(x, axis=0)
        new[3:6, at] = jnp.concatenate(v, axis=0)
        new[6:8, at] = own[6:8, at]

    columns_to_own(cols, rows, tab_i, store)


def force(cnt, win, rho, rho_h, own, mj, mr, ic, tab_j, tab_i):
    return call(
        force_kernel,
        "force",
        (cnt, win, rho, rho_h, own, mj, mr, ic, tab_j, tab_i),
        (0, 1),
        (WIDE, COLS, OWN),
        (pltpu.VMEM((1024, 8), F32), pltpu.VMEM((8, 1024), F32)),
    )


def pressure_kernel(cnt, rho, rho_h, tab_j, tab_i, mc, cc):
    pressure_tables(cnt, rho, rho_h, tab_j, tab_i, mc, cc)


def pressure_only(cnt, rho, rho_h, tab_j, tab_i):
    return call(pressure_kernel, "pressure", (cnt, rho, rho_h, tab_j, tab_i), (0,), (WIDE, COLS))


def first_kernel(cnt, win, grad, grad_h, rho, mj, mr, ic, mc, tab_j, tab_i, mg, gc, out, cols, rows):
    load = source(grad, grad_h)

    def fill(m, _):
        put(mg, m, gather(load, NJ, tab_j, m, NJ + m))
        return 0

    lax.fori_loop(0, cnt[0, 0], fill, 0)
    for k in range(NI):
        columns(gc, k, gather(load, NI, tab_i, k, NI + k))

    def body(m, picked, acc):
        xi, yi, zi, sx, sy, ux, uy, uz, ax, ay, az = picked
        dx, dy, dz, q = geometry(mj, mr, m, xi, yi, zi, sx, sy)
        q2 = q * q
        q3 = q2 * q
        bx, by, bz = row_of(mg, 0, m), row_of(mg, 1, m), row_of(mg, 2, m)
        dh = dx * (ax - bx) + dy * (ay - by) + dz * (az - bz)
        ub = (row_of(mj, 3, m) - ux) * bx + (row_of(mj, 4, m) - uy) * by + (row_of(mj, 5, m) - uz) * bz
        return (
            acc[0] + q2 * dh,
            acc[1] + q3 * ub,
            acc[2] + q3 * row_of(mc, 1, m),
            acc[3] + q3 * bx,
            acc[4] + q3 * by,
            acc[5] + q3 * bz,
        )

    pairs(cnt, win, body, [(ic, c) for c in GEO + (3, 4, 5)] + [(gc, 0), (gc, 1), (gc, 2)], cols, 6)

    def store(k, got):
        at = slice(128 * k, 128 * k + 128)
        held = live_of(tab_i, k)[0:1]
        p = jnp.where(held, rho[0:1, at], 1.0)
        inv = 1.0 / p
        inv2 = inv * inv
        by_coef = (-6.0 * MU) * got[0:1]
        by_pad = (0.5 * MU) * inv2 * got[1:2]
        g_rho = by_coef * (4.0 * inv2 - 8.0 * (p - 1.0) * inv2 * inv) + by_pad
        out[0:1, at] = jnp.where(held, 6.0 * g_rho, 0.0)
        out[1:4, at] = (-0.5 * MU) * (grad[0:3, at] * (got[2:3] * (1.0 / 3.0)) - inv * got[3:6])
        out[4:8, at] = jnp.zeros((4, 128), F32)

    columns_to_own(cols, rows, tab_i, store)


def first_sweep(*ins):
    return call(
        first_kernel,
        "adjoint1",
        ins,
        (0, 1),
        (WIDE, COLS, OWN),
        (pltpu.VMEM((1024, 8), F32), pltpu.VMEM((8, 1024), F32)),
    )


def second_kernel(final, cnt, win, part, part_h, carry, mj, mr, ic, mc, cc, mg, gc, tab_j, tab_i, grad, new, mp, pc, cols, rows):
    load = source(part, part_h)

    def fill(m, _):
        put(mp, m, gather(load, NJ, tab_j, m, NJ + m))
        return 0

    lax.fori_loop(0, cnt[0, 0], fill, 0)
    for k in range(NI):
        columns(pc, k, gather(load, NI, tab_i, k, NI + k))

    def body(m, picked, acc):
        xi, yi, zi, sx, sy, ux, uy, uz, ax, ay, az, ci, pi, ri = picked
        dx, dy, dz, q = geometry(mj, mr, m, xi, yi, zi, sx, sy)
        bx, by, bz = row_of(mg, 0, m), row_of(mg, 1, m), row_of(mg, 2, m)
        hx, hy, hz = ax - bx, ay - by, az - bz
        wx, wy, wz = row_of(mj, 3, m) - ux, row_of(mj, 4, m) - uy, row_of(mj, 5, m) - uz
        dh = dx * hx + dy * hy + dz * hz
        ua = wx * ax + wy * ay + wz * az
        ub = wx * bx + wy * by + wz * bz
        coef = ci + row_of(mc, 0, m)
        along = q * (q * (ua * row_of(mc, 1, m) - ub * pi + (ri + row_of(mp, 0, m))) - 4.0 * coef * dh)
        across = coef * (q * q)
        return (
            acc[0] + (along * dx + across * hx),
            acc[1] + (along * dy + across * hy),
            acc[2] + (along * dz + across * hz),
        )

    channels = [(ic, c) for c in GEO + (3, 4, 5)] + [(gc, 0), (gc, 1), (gc, 2), (cc, 0), (cc, 1), (pc, 0)]
    pairs(cnt, win, body, channels, cols, 3)

    def store(k, got):
        at = slice(128 * k, 128 * k + 128)
        gp = carry[0:3, at] + MU * got[0:3]
        gv = carry[3:6, at] + part[1:4, at]
        if not final:
            gv = gv + DT * gp
            held = live_of(tab_i, k)[0:3]
            grad[0:3, at] = jnp.where(held, DT * gv, 0.0)
            grad[3:8, at] = jnp.zeros((5, 128), F32)
        else:
            grad[:, at] = jnp.zeros((8, 128), F32)
        new[0:3, at] = gp
        new[3:6, at] = gv
        new[6:8, at] = jnp.zeros((2, 128), F32)

    columns_to_own(cols, rows, tab_i, store)


def second_sweep(final, *ins):
    return call(
        functools.partial(second_kernel, final),
        "adjoint2",
        ins,
        (0, 1),
        (OWN, OWN),
        (
            pltpu.VMEM((8, 4096), F32),
            pltpu.VMEM((1024, 8), F32),
            pltpu.VMEM((1024, 8), F32),
            pltpu.VMEM((8, 1024), F32),
        ),
    )


def tile_offsets():
    own = [(0, 0), (0, 1), (1, 0), (1, 1)]
    sides = [(-1, 0), (-1, 1), (2, 0), (2, 1), (0, -1), (1, -1), (0, 2), (1, 2)]
    corners = [(-1, -1), (2, -1), (-1, 2), (2, 2)]
    return own + sides + corners


def attributes():
    def edge(a):
        return {2: -0.5, -1: 0.5}.get(a, 0.0)

    wide = [[float(a), float(b), 0.0, 0.0, 0.0, 0.0, edge(a), edge(b)] for a, b in tile_offsets()]
    near = [[float(a), float(b), 0.0, 0.0, 0.0, 0.0, 2.0 * a - 1, 2.0 * b - 1] for a, b in tile_offsets()[:4]]
    attr_j = jnp.repeat(jnp.array(wide, F32).T, 256, axis=1)
    attr_i = jnp.repeat(jnp.array(near, F32).T, 256, axis=1)
    return attr_j, attr_i


def per_device(nx, ny, positions, velocities, occupancy, cot_positions, cot_velocities):
    flat = lambda a: a.reshape(3, 1024)
    slots = lax.broadcasted_iota(I32, (2, 2, 256), 2)
    live = (slots < occupancy[:, :, None]).astype(F32).reshape(1, 1024)
    zero = jnp.zeros((1, 1024), F32)
    state = jnp.concatenate(
        [flat(positions), flat(velocities), live, zero, flat(cot_positions), flat(cot_velocities), zero, zero], axis=0
    )
    there = [(a * ny + b, logical_to_mesh(a, b)) for a in range(nx) for b in range(ny)]
    there = [(s, d[0] * ny + d[1]) for s, d in there]
    state = lax.ppermute(state, ("gx", "gy"), there)
    _, gy = mesh_to_logical(lax.axis_index("gx"), lax.axis_index("gy"))
    lane = lax.broadcasted_iota(I32, (1, 3072), 1)
    lower = ((lane >= 1024) & (lane < 1536)) | ((lane >= 2048) & (lane < 2560))
    upper = ((lane >= 1536) & (lane < 2048)) | (lane >= 2560)
    ok = jnp.where((lower & (gy == 0)) | (upper & (gy == ny - 1)), 0.0, 1.0)
    grad_vel = state[11:14] + DT * state[8:11]
    grad = DT * state[6:7] * grad_vel
    pad2 = jnp.zeros((2, 1024), F32)
    carry = jnp.concatenate([state[8:11], grad_vel, pad2], axis=0)
    own = state[0:8]
    start = jnp.concatenate([own, grad, jnp.zeros((5, 1024), F32)], axis=0)
    attr_j, attr_i = attributes()

    hal16 = halo(start, nx, ny, 1)
    hal = hal16[0:8]
    grad, grad_h = start[8:16], hal16[8:16]
    tab_j, tab_i, cnt = plan(own, hal, ok)
    history = []
    for step in range(STEPS):
        if step:
            hal = halo(own, nx, ny, 0)
        mj, mr, ic, win, rho = density(cnt, own, hal, attr_j, attr_i, tab_j, tab_i)
        rho_h = halo(rho, nx, ny, 0)
        if step + 1 < STEPS:
            mc, cc, own = force(cnt, win, rho, rho_h, own, mj, mr, ic, tab_j, tab_i)
        else:
            mc, cc = pressure_only(cnt, rho, rho_h, tab_j, tab_i)
        history.append((win, rho, mj, mr, ic, mc, cc))
    for step in reversed(range(STEPS)):
        win, rho, mj, mr, ic, mc, cc = history[step]
        mg, gc, part = first_sweep(cnt, win, grad, grad_h, rho, mj, mr, ic, mc, tab_j, tab_i)
        part_h = halo(part, nx, ny, 0)
        grad, carry = second_sweep(step == 0, cnt, win, part, part_h, carry, mj, mr, ic, mc, cc, mg, gc, tab_j, tab_i)
        if step:
            grad_h = halo(grad, nx, ny, 0)
    back = [(d, s) for s, d in there]
    result = lax.ppermute(carry, ("gx", "gy"), back)
    return result[0:3].reshape(positions.shape), result[3:6].reshape(positions.shape)


def solution(mesh):
    spec = P(None, "gx", "gy", None)
    return jax.shard_map(
        functools.partial(per_device, mesh.shape["gx"], mesh.shape["gy"]),
        mesh=mesh,
        in_specs=(spec, spec, P("gx", "gy"), spec, spec),
        out_specs=(spec, spec),
        check_vma=False,
    )
```

profile of v0, /device:TPU:58, one launch (start us, length us, event | category | flops | bytes accessed | tf_op | source)
XLA Modules:
  0.0 297.5 jit_solution(11841798604291499852)
XLA Ops:
  3.7 9.0 %collective-permute-start = (f32[16,1024]{1,0:T(8,128)S(1)}, f32[16,1024]{1,0:T(8,128)S(1)}, u32[]{:S(2)}, u32[]{:S(2)}) collective-permute-start(f32[16,1024]{1,0:T(8,128)S(1)} %concatenate.12), channel_id=1, source_target_pairs={{0,0},{1,1},{2,33},{3,32},{4,4},{5,5},{6,37},{7,36},{8,8},{9,9},{1... | collective-permute-start | bytes 196616 | tf_op jit(solution)/shard_map/ppermute | solution.py:621
  26.8 9.0 %density.4 = (f32[8,4096]{1,0:T(8,128)S(1)}, f32[32,128]{1,0:T(8,128)S(1)}, f32[1024,8]{1,0:T(8,128)S(1)}, s32[8,128]{1,0:T(8,128)S(1)}, f32[8,1024]{1,0:T(8,128)S(1)}) custom-call(s32[1,128]{1,0:T(1,128)S(1)} %get-tuple-element.55.cnt, f32[8,1024]{1,0:T(8,128)S(1)} %slice.35.own, f32[8,3072]{1,0:T(8,128)S(1)} %get-tuple-element.111.hal, ...), custom_call_target="tpu_custom_call" | custom-call | tf_op jit(solution)/shard_map/density/pallas_call | solution.py:365
  42.8 10.1 %force.3 = (f32[8,4096]{1,0:T(8,128)S(1)}, f32[1024,8]{1,0:T(8,128)S(1)}, f32[8,1024]{1,0:T(8,128)S(1)}) custom-call(s32[1,128]{1,0:T(1,128)S(1)} %get-tuple-element.55.cnt, s32[8,128]{1,0:T(8,128)S(1)} %get-tuple-element.58.win, f32[8,1024]{1,0:T(8,128)S(1)} %get-tuple-element.59.src.rho, f32[8,3072]{1,0:T(8,128)S(1)} %halo8.14.rho_h, ...), custom_call_target="tpu_custom_call" | custom-call | tf_op jit(solution)/shard_map/force/pallas_call | solution.py:365
  58.4 9.1 %density.5 = (f32[8,4096]{1,0:T(8,128)S(1)}, f32[32,128]{1,0:T(8,128)S(1)}, f32[1024,8]{1,0:T(8,128)S(1)}, s32[8,128]{1,0:T(8,128)S(1)}, f32[8,1024]{1,0:T(8,128)S(1)}) custom-call(s32[1,128]{1,0:T(1,128)S(1)} %get-tuple-element.55.cnt, f32[8,1024]{1,0:T(8,128)S(1)} %get-tuple-element.63.src.own, f32[8,3072]{1,0:T(8,128)S(1)} %halo8.15.hal, ...), custom_call_target="tpu_custom_call" | custom-call | tf_op jit(solution)/shard_map/density/pallas_call | solution.py:365
  73.0 10.2 %force.4 = (f32[8,4096]{1,0:T(8,128)S(1)}, f32[1024,8]{1,0:T(8,128)S(1)}, f32[8,1024]{1,0:T(8,128)S(1)}) custom-call(s32[1,128]{1,0:T(1,128)S(1)} %get-tuple-element.55.cnt, s32[8,128]{1,0:T(8,128)S(1)} %get-tuple-element.64.win, f32[8,1024]{1,0:T(8,128)S(1)} %get-tuple-element.65.src.rho, f32[8,3072]{1,0:T(8,128)S(1)} %halo8.16.rho_h, ...), custom_call_target="tpu_custom_call" | custom-call | tf_op jit(solution)/shard_map/force/pallas_call | solution.py:365
  88.6 9.1 %density.6 = (f32[8,4096]{1,0:T(8,128)S(1)}, f32[32,128]{1,0:T(8,128)S(1)}, f32[1024,8]{1,0:T(8,128)S(1)}, s32[8,128]{1,0:T(8,128)S(1)}, f32[8,1024]{1,0:T(8,128)S(1)}) custom-call(s32[1,128]{1,0:T(1,128)S(1)} %get-tuple-element.55.cnt, f32[8,1024]{1,0:T(8,128)S(1)} %get-tuple-element.69.src.own, f32[8,3072]{1,0:T(8,128)S(1)} %halo8.17.hal, ...), custom_call_target="tpu_custom_call" | custom-call | tf_op jit(solution)/shard_map/density/pallas_call | solution.py:365
  103.2 10.2 %force.5 = (f32[8,4096]{1,0:T(8,128)S(1)}, f32[1024,8]{1,0:T(8,128)S(1)}, f32[8,1024]{1,0:T(8,128)S(1)}) custom-call(s32[1,128]{1,0:T(1,128)S(1)} %get-tuple-element.55.cnt, s32[8,128]{1,0:T(8,128)S(1)} %get-tuple-element.70.win, f32[8,1024]{1,0:T(8,128)S(1)} %get-tuple-element.71.src.rho, f32[8,3072]{1,0:T(8,128)S(1)} %halo8.18.rho_h, ...), custom_call_target="tpu_custom_call" | custom-call | tf_op jit(solution)/shard_map/force/pallas_call | solution.py:365
  119.2 9.1 %density.7 = (f32[8,4096]{1,0:T(8,128)S(1)}, f32[32,128]{1,0:T(8,128)S(1)}, f32[1024,8]{1,0:T(8,128)S(1)}, s32[8,128]{1,0:T(8,128)S(1)}, f32[8,1024]{1,0:T(8,128)S(1)}) custom-call(s32[1,128]{1,0:T(1,128)S(1)} %get-tuple-element.55.cnt, f32[8,1024]{1,0:T(8,128)S(1)} %get-tuple-element.75.src.own, f32[8,3072]{1,0:T(8,128)S(1)} %halo8.19.hal, ...), custom_call_target="tpu_custom_call" | custom-call | tf_op jit(solution)/shard_map/density/pallas_call | solution.py:365
  137.1 11.3 %adjoint1.4 = (f32[8,4096]{1,0:T(8,128)S(1)}, f32[1024,8]{1,0:T(8,128)S(1)}, f32[8,1024]{1,0:T(8,128)S(1)}) custom-call(s32[1,128]{1,0:T(1,128)S(1)} %get-tuple-element.55.cnt, s32[8,128]{1,0:T(8,128)S(1)} %get-tuple-element.76.win, f32[8,1024]{1,0:T(8,128)S(1)} %concatenate.14.grad, f32[8,3072]{1,0:T(8,128)S(1)} %get-tuple-element.110.grad_h, ...), custom_call_target="tpu_custom_call" | custom-call | tf_op jit(solution)/shard_map/adjoint1/pallas_call | solution.py:365
  148.4 8.0 %halo8.21.part_h = f32[8,3072]{1,0:T(8,128)S(1)} custom-call(f32[8,1024]{1,0:T(8,128)S(1)} %get-tuple-element.82.src.part), custom_call_target="tpu_custom_call" | custom-call | tf_op jit(solution)/shard_map/halo8/pallas_call | solution.py:122
  156.5 12.0 %adjoint2.4 = (f32[8,1024]{1,0:T(8,128)S(1)}, f32[8,1024]{1,0:T(8,128)S(1)}) custom-call(s32[1,128]{1,0:T(1,128)S(1)} %get-tuple-element.55.cnt, s32[8,128]{1,0:T(8,128)S(1)} %get-tuple-element.76.win, f32[8,1024]{1,0:T(8,128)S(1)} %get-tuple-element.82.src.part, f32[8,3072]{1,0:T(8,128)S(1)} %halo8.21.part_h, f32[8,1024]{1,0:T(8,128)S(1)} %pad_maximum_fusion.carry, ...), custom_call_target="tpu_custom_call" | custom-call | tf_op jit(solution)/shard_map/adjoint2/pallas_call | solution.py:365
  168.5 7.9 %halo8.22.grad_h = f32[8,3072]{1,0:T(8,128)S(1)} custom-call(f32[8,1024]{1,0:T(8,128)S(1)} %get-tuple-element.86.src.grad), custom_call_target="tpu_custom_call" | custom-call | tf_op jit(solution)/shard_map/halo8/pallas_call | solution.py:122
  176.4 11.2 %adjoint1.5 = (f32[8,4096]{1,0:T(8,128)S(1)}, f32[1024,8]{1,0:T(8,128)S(1)}, f32[8,1024]{1,0:T(8,128)S(1)}) custom-call(s32[1,128]{1,0:T(1,128)S(1)} %get-tuple-element.55.cnt, s32[8,128]{1,0:T(8,128)S(1)} %get-tuple-element.70.win, f32[8,1024]{1,0:T(8,128)S(1)} %get-tuple-element.86.src.grad, f32[8,3072]{1,0:T(8,128)S(1)} %halo8.22.grad_h, ...), custom_call_target="tpu_custom_call" | custom-call | tf_op jit(solution)/shard_map/adjoint1/pallas_call | solution.py:365
  187.5 7.4 %halo8.23.part_h = f32[8,3072]{1,0:T(8,128)S(1)} custom-call(f32[8,1024]{1,0:T(8,128)S(1)} %get-tuple-element.88.src.part), custom_call_target="tpu_custom_call" | custom-call | tf_op jit(solution)/shard_map/halo8/pallas_call | solution.py:122
  194.9 11.9 %adjoint2.5 = (f32[8,1024]{1,0:T(8,128)S(1)}, f32[8,1024]{1,0:T(8,128)S(1)}) custom-call(s32[1,128]{1,0:T(1,128)S(1)} %get-tuple-element.55.cnt, s32[8,128]{1,0:T(8,128)S(1)} %get-tuple-element.70.win, f32[8,1024]{1,0:T(8,128)S(1)} %get-tuple-element.88.src.part, f32[8,3072]{1,0:T(8,128)S(1)} %halo8.23.part_h, f32[8,1024]{1,0:T(8,128)S(1)} %get-tuple-element.89.carry, ...), custom_call_target="tpu_custom_call" | custom-call | tf_op jit(solution)/shard_map/adjoint2/pallas_call | solution.py:365
  206.9 7.6 %halo8.24.grad_h = f32[8,3072]{1,0:T(8,128)S(1)} custom-call(f32[8,1024]{1,0:T(8,128)S(1)} %get-tuple-element.93.src.grad), custom_call_target="tpu_custom_call" | custom-call | tf_op jit(solution)/shard_map/halo8/pallas_call | solution.py:122
  214.5 11.2 %adjoint1.6 = (f32[8,4096]{1,0:T(8,128)S(1)}, f32[1024,8]{1,0:T(8,128)S(1)}, f32[8,1024]{1,0:T(8,128)S(1)}) custom-call(s32[1,128]{1,0:T(1,128)S(1)} %get-tuple-element.55.cnt, s32[8,128]{1,0:T(8,128)S(1)} %get-tuple-element.64.win, f32[8,1024]{1,0:T(8,128)S(1)} %get-tuple-element.93.src.grad, f32[8,3072]{1,0:T(8,128)S(1)} %halo8.24.grad_h, ...), custom_call_target="tpu_custom_call" | custom-call | tf_op jit(solution)/shard_map/adjoint1/pallas_call | solution.py:365
  225.7 7.2 %halo8.25.part_h = f32[8,3072]{1,0:T(8,128)S(1)} custom-call(f32[8,1024]{1,0:T(8,128)S(1)} %get-tuple-element.95.src.part), custom_call_target="tpu_custom_call" | custom-call | tf_op jit(solution)/shard_map/halo8/pallas_call | solution.py:122
  232.9 11.9 %adjoint2.6 = (f32[8,1024]{1,0:T(8,128)S(1)}, f32[8,1024]{1,0:T(8,128)S(1)}) custom-call(s32[1,128]{1,0:T(1,128)S(1)} %get-tuple-element.55.cnt, s32[8,128]{1,0:T(8,128)S(1)} %get-tuple-element.64.win, f32[8,1024]{1,0:T(8,128)S(1)} %get-tuple-element.95.src.part, f32[8,3072]{1,0:T(8,128)S(1)} %halo8.25.part_h, f32[8,1024]{1,0:T(8,128)S(1)} %get-tuple-element.96.carry, ...), custom_call_target="tpu_custom_call" | custom-call | tf_op jit(solution)/shard_map/adjoint2/pallas_call | solution.py:365
  244.8 7.4 %halo8.26.grad_h = f32[8,3072]{1,0:T(8,128)S(1)} custom-call(f32[8,1024]{1,0:T(8,128)S(1)} %get-tuple-element.100.src.grad), custom_call_target="tpu_custom_call" | custom-call | tf_op jit(solution)/shard_map/halo8/pallas_call | solution.py:122
  252.2 11.1 %adjoint1.7 = (f32[8,4096]{1,0:T(8,128)S(1)}, f32[1024,8]{1,0:T(8,128)S(1)}, f32[8,1024]{1,0:T(8,128)S(1)}) custom-call(s32[1,128]{1,0:T(1,128)S(1)} %get-tuple-element.55.cnt, s32[8,128]{1,0:T(8,128)S(1)} %get-tuple-element.58.win, f32[8,1024]{1,0:T(8,128)S(1)} %get-tuple-element.100.src.grad, f32[8,3072]{1,0:T(8,128)S(1)} %halo8.26.grad_h, ...), custom_call_target="tpu_custom_call" | custom-call | tf_op jit(solution)/shard_map/adjoint1/pallas_call | solution.py:365
  263.4 7.3 %halo8.27.part_h = f32[8,3072]{1,0:T(8,128)S(1)} custom-call(f32[8,1024]{1,0:T(8,128)S(1)} %get-tuple-element.102.src.part), custom_call_target="tpu_custom_call" | custom-call | tf_op jit(solution)/shard_map/halo8/pallas_call | solution.py:122
  270.7 12.1 %adjoint2.7 = (f32[8,1024]{1,0:T(8,128)}, f32[8,1024]{1,0:T(8,128)S(1)}) custom-call(s32[1,128]{1,0:T(1,128)S(1)} %get-tuple-element.55.cnt, s32[8,128]{1,0:T(8,128)S(1)} %get-tuple-element.58.win, f32[8,1024]{1,0:T(8,128)S(1)} %get-tuple-element.102.src.part, f32[8,3072]{1,0:T(8,128)S(1)} %halo8.27.part_h, f32[8,1024]{1,0:T(8,128)S(1)} %get-tuple-element.103.carry, ...), custom_call_target="tpu_custom_call" | custom-call | tf_op jit(solution)/shard_map/adjoint2/pallas_call | solution.py:365
  282.8 11.9 %collective-permute-start.1 = (f32[8,1024]{1,0:T(8,128)S(1)}, f32[8,1024]{1,0:T(8,128)S(1)}, u32[]{:S(2)}, u32[]{:S(2)}) collective-permute-start(f32[8,1024]{1,0:T(8,128)S(1)} %get-tuple-element.107), channel_id=1, source_target_pairs={{0,0},{1,1},{33,2},{32,3},{4,4},{5,5},{37,6},{36,7},{8,8},{9,9},{4... | collective-permute-start | bytes 98312 | tf_op jit(solution)/shard_map/ppermute | solution.py:658
  (48 shorter events, 63.3 us)
Async XLA Ops:
  0.6 0.8 copy-start
  1.4 0.7 copy-start.1
  2.1 0.7 copy-start.2
  2.8 0.7 copy-start.3
  3.7 14.1 %collective-permute-start = (f32[16,1024]{1,0:T(8,128)S(1)}, f32[16,1024]{1,0:T(8,128)S(1)}, u32[]{:S(2)}, u32[]{:S(2)}) collective-permute-start(f32[16,1024]{1,0:T(8,128)S(1)} %concatenate.12), channel_id=1, source_target_pairs={{0,0},{1,1},{2,33},{3,32},{4,4},{5,5},{6,37},{7,36},{8,8},{9,9},{1... | collective-permute-start | bytes 196616 | tf_op jit(solution)/shard_map/ppermute | solution.py:621
  23.9 2.1 copy-start.5
  26.1 0.7 copy-start.4
  282.8 13.5 %collective-permute-start.1 = (f32[8,1024]{1,0:T(8,128)S(1)}, f32[8,1024]{1,0:T(8,128)S(1)}, u32[]{:S(2)}, u32[]{:S(2)}) collective-permute-start(f32[8,1024]{1,0:T(8,128)S(1)} %get-tuple-element.107), channel_id=1, source_target_pairs={{0,0},{1,1},{33,2},{32,3},{4,4},{5,5},{37,6},{36,7},{8,8},{9,9},{4... | collective-permute-start | bytes 98312 | tf_op jit(solution)/shard_map/ppermute | solution.py:658
where the time goes:
time: 303 us; the launch traced here: 298 us
  Pallas kernels  264 us (87%)
  starting transfers between devices  20.9 us (7%)
  waiting for transfers between devices  6.52 us (2%)
  local copies, waits for them, and re-layouts  4.36 us (1%)
    pallas_call x16, Pallas kernels, call(): pl.pallas_call(kernel, out_shape=tuple((jax.ShapeDtypeStruct(s, t) for s,...  162 us
    pallas_call x15, Pallas kernels, halo(): pl.pallas_call(functools.partial(halo_kernel, nx, ny), out_shape=jax.Shap...  99.6 us
    ppermute x1, starting transfers between devices, per_device(): result = lax.ppermute(carry, ('gx', 'gy'), back)  11.9 us
    ppermute x1, starting transfers between devices, per_device(): state = lax.ppermute(state, ('gx', 'gy'), there)  8.97 us
  transfers between devices with their start and end apart: 2, of which 2 were waited for; matrix products, arithmetic and copies ran while one was open for 0% of the time, Pallas kernels for 0%

commit v1 on v0

v1 whole, which is shorter than its diff:
```python
import functools

import jax
import jax.numpy as jnp
from jax import lax
from jax.experimental import pallas as pl
from jax.experimental.pallas import tpu as pltpu
from jax.sharding import PartitionSpec as P

STEPS = 4
DT = 0.05
MU = 0.15
MESH = pl.DeviceIdType.MESH
F32 = jnp.float32
I32 = jnp.int32
NJ, NI = 32, 8
NK = 30
SB = 32
NS = 128
REACH = 1.0001


def logical_to_mesh(column, half):
    y = column // 32
    s = column % 32
    s = s + (y % 2) * (31 - 2 * s)
    z = s // 4
    x = s % 4
    x = x + (z % 2) * (3 - 2 * x)
    return (y * 2 + x % 2) * 8 + z, (x // 2) * 2 + half


def mesh_to_logical(gx, gy):
    y = gx // 16
    z = gx % 8
    x = (gy // 2) * 2 + (gx // 8) % 2
    s = 4 * z + x + (z % 2) * (3 - 2 * x)
    return 32 * y + s + (y % 2) * (31 - 2 * s), gy % 2


def halo_kernel(ring, src, out, send_sem, recv_sem):
    column, half = mesh_to_logical(lax.axis_index("gx"), lax.axis_index("gy"))
    left, right, other = (column + ring - 1) % ring, (column + 1) % ring, 1 - half
    barrier = pltpu.get_barrier_semaphore()
    for who in ((left, half), (right, half), (left, other), (right, other), (column, other)):
        pl.semaphore_signal(barrier, inc=1, device_id=logical_to_mesh(*who), device_id_type=MESH)
    pl.semaphore_wait(barrier, 5)
    rim = pl.multiple_of(768 * other, 128)

    def copy(k, start, dest, n, who):
        return pltpu.make_async_remote_copy(
            src_ref=src.at[:, pl.ds(start, n)],
            dst_ref=out.at[:, pl.ds(dest, n)],
            send_sem=send_sem.at[k],
            recv_sem=recv_sem.at[k],
            device_id=logical_to_mesh(*who),
            device_id_type=MESH,
        )

    copies = [
        copy(0, rim, 2304, 256, (right, other)),
        copy(1, rim, 2560, 256, (left, other)),
        copy(2, 0, 0, 1024, (right, half)),
        copy(3, 0, 1024, 1024, (left, half)),
        copy(4, rim, 2048, 256, (column, other)),
    ]
    for c in copies:
        c.start()
    for c in copies:
        c.wait()


VM = pl.BlockSpec(memory_space=pltpu.VMEM)
SM = pl.BlockSpec(memory_space=pltpu.SMEM)


def halo(own, ring, cid):
    rows = own.shape[0]
    return pl.pallas_call(
        functools.partial(halo_kernel, ring),
        out_shape=jax.ShapeDtypeStruct((rows, 3072), F32),
        in_specs=[VM],
        out_specs=VM,
        scratch_shapes=[pltpu.SemaphoreType.DMA((5,)), pltpu.SemaphoreType.DMA((5,))],
        compiler_params=pltpu.CompilerParams(
            collective_id=cid, has_side_effects=True, vmem_limit_bytes=2 << 20
        ),
        name=f"halo{rows}",
    )(own)


def iota(shape, dim):
    return lax.broadcasted_iota(I32, shape, dim)


def dot_t(a, b):
    return lax.dot_general(a, b, (((1,), (1,)), ((), ())), preferred_element_type=F32)


def plan_kernel(own, hal, tab_j, tab_i, cnt, pre):
    sub = iota((NS, 128), 0)
    lane = iota((NS, 128), 1)
    upper = jnp.where(sub <= lane, 1.0, 0.0).astype(jnp.bfloat16)
    strict = jnp.where(lane < sub, 1.0, 0.0)

    def row(k):
        if k < NI:
            z = own[2:3, 128 * k : 128 * k + 128]
            live = own[6:7, 128 * k : 128 * k + 128] > 0.5
        else:
            s = 128 * (k - NI)
            z = hal[2:3, s : s + 128]
            live = hal[6:7, s : s + 128] > 0.5
        bucket = jnp.clip((z * 8.0).astype(I32), 0, NS - 1)
        return jnp.where(live, bucket, -1)

    carry = jnp.zeros((NS, 1), F32)
    total_i = carry
    for k in range(NK):
        hot = jnp.where(sub == row(k), 1.0, 0.0)
        count = jnp.dot(hot.astype(jnp.bfloat16), upper, preferred_element_type=F32)
        pre[:, 128 * k : 128 * k + 128] = count + carry - 1.0
        carry = carry + count[:, 127:128]
        if k == NI - 1:
            total_i = carry
    hi = lax.Precision.HIGHEST
    off_j = jnp.dot(strict, jnp.broadcast_to(carry, (NS, 128)), precision=hi, preferred_element_type=F32)
    off_i = jnp.dot(strict, jnp.broadcast_to(total_i, (NS, 128)), precision=hi, preferred_element_type=F32)

    def inverse(blocks, offset, nh, k, acc):
        b = row(k)
        rank = jnp.sum(
            jnp.where(sub == b, pre[:, 128 * k : 128 * k + 128] + offset, 0.0), axis=0, keepdims=True
        ).astype(I32)
        rank = jnp.where(b >= 0, rank, -128)
        high, low = rank >> 7, rank & 127
        eq = iota((nh, 128), 0) == high
        a = jnp.concatenate(
            [jnp.where(eq, iota((nh, 128), 1), 0), jnp.where(eq, k + 1, 0)], axis=0
        ).astype(F32).astype(jnp.bfloat16)
        hot = jnp.where(sub == low, 1.0, 0.0).astype(jnp.bfloat16)
        return acc + dot_t(a, hot), high, low

    acc = jnp.zeros((2 * NJ, 128), F32)
    for k in range(NK):
        acc, _, _ = inverse(NJ, off_j, NJ, k, acc)
    tab_j[0:NJ, :] = acc[0:NJ].astype(I32)
    tab_j[NJ : 2 * NJ, :] = acc[NJ:].astype(I32) - 1
    acc = jnp.zeros((2 * NI, 128), F32)
    for k in range(NI):
        acc, high, low = inverse(NI, off_i, NI, k, acc)
        tab_i[16 + k : 17 + k, :] = high
        tab_i[24 + k : 25 + k, :] = jnp.maximum(low, 0)
    tab_i[0:NI, :] = acc[0:NI].astype(I32)
    tab_i[NI : 2 * NI, :] = acc[NI:].astype(I32) - 1
    nj = jnp.sum(carry, axis=0, keepdims=True)
    ni = jnp.sum(total_i, axis=0, keepdims=True)
    at = iota((1, 128), 1)
    blocks_j = (nj + 127.0).astype(I32) >> 7
    groups_i = (ni + (SB - 1.0)).astype(I32) >> 5
    cnt[...] = jnp.where(at == 0, blocks_j, groups_i)


def plan(own, hal):
    return pl.pallas_call(
        plan_kernel,
        out_shape=(
            jax.ShapeDtypeStruct((2 * NJ, 128), I32),
            jax.ShapeDtypeStruct((32, 128), I32),
            jax.ShapeDtypeStruct((1, 128), I32),
        ),
        in_specs=[VM] * 2,
        out_specs=(VM, VM, VM),
        scratch_shapes=[pltpu.VMEM((NS, 4096), F32)],
        compiler_params=pltpu.CompilerParams(vmem_limit_bytes=8 << 20),
        name="plan",
    )(own, hal)


def take(block, idx):
    return jnp.take_along_axis(block, idx, axis=1, mode="promise_in_bounds")


def gather(load, count, table, lane_row, blk_row):
    idx = jnp.broadcast_to(table[pl.ds(lane_row, 1), :], (8, 128))
    blk = jnp.broadcast_to(table[pl.ds(blk_row, 1), :], (8, 128))
    out = jnp.zeros((8, 128), F32)
    for k in range(count):
        out = jnp.where(blk == k, take(load(k), idx), out)
    return out


def spread(own, hal, stage, n):
    for k in range(NK):
        part = own[:, 128 * k : 128 * k + 128] if k < NI else hal[:, 128 * (k - NI) : 128 * (k - NI) + 128]
        for c in range(n):
            stage[NJ * c + k : NJ * c + k + 1, :] = part[c : c + 1]


def pick(stage, c, groups, idx, blk):
    sub = iota((8, 128), 0)
    out = jnp.zeros((8, 128), F32)
    for j in range(groups):
        part = stage[NJ * c + 8 * j : NJ * c + 8 * j + 8, :]
        out = jnp.where(blk == sub + 8 * j, take(part, idx), out)
    return jnp.sum(out, axis=0, keepdims=True)


def entry(table, lane_row, blk_row):
    idx = jnp.broadcast_to(table[pl.ds(lane_row, 1), :], (8, 128))
    return idx, jnp.broadcast_to(table[pl.ds(blk_row, 1), :], (8, 128))


def each_block(cnt, fill, together=8):
    def several(b, _):
        for n in range(together):
            fill(together * b + n, 0)
        return 0

    lax.fori_loop(0, (cnt[0, 0] + together - 1) // together, several, 0)


def block(ref, m):
    return ref[:, pl.ds(pl.multiple_of(m * 128, 128), 128)]


def put(ref, m, value):
    ref[:, pl.ds(pl.multiple_of(m * 128, 128), 128)] = value


def columns(ref, k, rows):
    ref[128 * k : 128 * k + 128, :] = rows.T


def sums_to_own(cnt, sums, n_out, cols, rows, tab_i, store):
    def reduce(b, _):
        for n in range(4):
            at = pl.multiple_of(b * 512 + 128 * n, 128)
            for c in range(n_out):
                cols[pl.ds(at, 128), c : c + 1] = jnp.sum(sums[c, pl.ds(at, 128), :], axis=1, keepdims=True)
        for n in range(4):
            at = pl.multiple_of(b * 512 + 128 * n, 128)
            rows[:, pl.ds(at, 128)] = cols[pl.ds(at, 128), :].T
        return 0

    lax.fori_loop(0, (cnt[0, 1] + 15) >> 4, reduce, 0)
    load = lambda m: rows[:, 128 * m : 128 * m + 128]
    for k in range(NI):
        store(k, gather(load, NI, tab_i, 24 + k, 16 + k))


def broadcast_columns(cnt, channels, sums, n_out):
    def one(b, _):
        at = pl.multiple_of(b * 128, 128)
        for ref, c, wide, n in channels:
            wide[n, pl.ds(at, 128), :] = jnp.broadcast_to(ref[pl.ds(at, 128), c : c + 1], (128, 128))
        for c in range(n_out):
            sums[c, pl.ds(at, 128), :] = jnp.zeros((128, 128), F32)
        return 0

    lax.fori_loop(0, (cnt[0, 1] + 3) >> 2, one, 0)


def pairs(cnt, win, rows, body, mine, sums):
    def each(m, _):
        picked = rows(m)
        first = win[m, 0]

        def chunk(n, _):
            at = pl.multiple_of((first + 4 * n) * 8, 8)
            terms = body(picked, *[wide[c, pl.ds(at, SB), :] for wide, c in mine])
            for c, term in enumerate(terms):
                sums[c, pl.ds(at, SB), :] += term
            return 0

        lax.fori_loop(0, win[m, 1], chunk, 0)
        return 0

    lax.fori_loop(0, cnt[0, 0], each, 0)


def places(*refs):
    return [(ref, c) for ref, count in refs for c in range(count)]


def row_of(ref, c, m):
    return ref[c : c + 1, pl.ds(pl.multiple_of(m * 128, 128), 128)]


def spot(mj, m):
    return [row_of(mj, c, m) for c in GEO]


def geometry(spots, xi, yi, zi, bi):
    xj, yj, zj, bj = [jnp.broadcast_to(r, (SB, 128)) for r in spots]
    dx, dy, dz, db = xj - xi, yj - yi, zj - zi, bj - bi
    top = jnp.minimum(2.0 - db * db, 1.0)
    q = jnp.maximum(top - (dx * dx + dy * dy + dz * dz), 0.0)
    return dx, dy, dz, q


GEO = (0, 1, 2, 6)


def live_of(tab_i, k):
    return jnp.broadcast_to(tab_i[16 + k : 17 + k, :], (8, 128)) >= 0


def density_kernel(cnt, own, hal, attr_j, attr_i, tab_j, tab_i, mj, ic, win, rho, geo, cols, rows, zlo, zhi, win_s, sem, stage, sums):
    body6 = iota((8, 128), 0) < 6
    for k in range(NK):
        part = own[0:8, 128 * k : 128 * k + 128] if k < NI else hal[0:8, 128 * (k - NI) : 128 * (k - NI) + 128]
        stage[:, 128 * k : 128 * k + 128] = jnp.where(body6, part, 0.0) + attr_j[:, 128 * k : 128 * k + 128]
    load = lambda k: stage[:, 128 * k : 128 * k + 128]
    zlo[...] = jnp.full((NJ, 128), 1e30, F32)
    zhi[...] = jnp.full((NJ, 128), -1e30, F32)

    def fill(m, _):
        got = gather(load, NK, tab_j, m, NJ + m)
        held = tab_j[pl.ds(NJ + m, 1), :] >= 0
        put(mj, m, jnp.where((iota((8, 128), 0) == 6) & ~held, 1000.0, got))
        zlo[pl.ds(m, 1), :] = jnp.where(held, got[2:3], 1e30)
        zhi[pl.ds(m, 1), :] = jnp.where(held, got[2:3], -1e30)
        return 0

    each_block(cnt, fill, 4)
    body6 = iota((8, 128), 0) < 6

    def load_i(k):
        at = slice(128 * k, 128 * k + 128)
        return jnp.where(body6, own[:, at], 0.0) + attr_i[:, at]

    z_rows = []
    for k in range(NI):
        got = gather(load_i, NI, tab_i, k, NI + k)
        columns(ic, k, got)
        z_rows.append(got[2:3])
    low = jnp.min(zlo[...], axis=1, keepdims=True) - REACH
    high = jnp.max(zhi[...], axis=1, keepdims=True) + REACH
    first = jnp.full((NJ, 128), 4096, I32)
    last = jnp.zeros((NJ, 128), I32)
    for k in range(NI):
        held = tab_i[NI + k : NI + k + 1, :] >= 0
        meets = (z_rows[k] > low) & (z_rows[k] < high) & held
        at = iota((NJ, 128), 1) + 128 * k
        first = jnp.minimum(first, jnp.where(meets, at, 4096))
        last = jnp.maximum(last, jnp.where(meets, at + 1, 0))
    first = jnp.min(first.astype(F32), axis=1, keepdims=True).astype(I32) >> 3
    last = jnp.max(last.astype(F32), axis=1, keepdims=True).astype(I32)
    chunks = jnp.maximum(last - 8 * first + (SB - 1), 0) >> 5
    windows = jnp.where(iota((NJ, 128), 1) == 0, first, chunks)
    win[...] = windows
    copy = pltpu.make_async_copy(win, win_s, sem)
    copy.start()
    broadcast_columns(cnt, [(ic, c, geo, n) for n, c in enumerate(GEO)], sums, 1)
    copy.wait()

    def body(spots, *mine):
        _, _, _, q = geometry(spots, *mine)
        return (q * q * q,)

    pairs(cnt, win_s, lambda m: spot(mj, m), body, places((geo, 4)), sums)

    def store(k, got):
        rho[:, 128 * k : 128 * k + 128] = MU * got[0:1]

    sums_to_own(cnt, sums, 1, cols, rows, tab_i, store)


def call(kernel, name, ins, smem, outs, scratch=()):
    specs = [SM if i in smem else VM for i in range(len(ins))]
    return pl.pallas_call(
        kernel,
        out_shape=tuple(jax.ShapeDtypeStruct(s, t) for s, t in outs),
        in_specs=specs,
        out_specs=tuple(VM for _ in outs),
        scratch_shapes=list(scratch),
        compiler_params=pltpu.CompilerParams(vmem_limit_bytes=12 << 20),
        name=name,
    )(*ins)


def scratch(n_in, n_out):
    return (
        pltpu.VMEM((1024, 8), F32),
        pltpu.VMEM((8, 1024), F32),
        pltpu.VMEM((8 * NJ, 128), F32),
        pltpu.VMEM((n_in, 1024 + SB, 128), F32),
        pltpu.VMEM((n_out, 1024 + SB, 128), F32),
    )


COLS = ((1024, 8), F32)
OWN = ((8, 1024), F32)
ROW = ((1, 1024), F32)


def lanes(n):
    return ((n, 1024 + SB, 128), F32)


GRAD = ((4, 1024), F32)
WIDE = ((8, 4096), F32)


def density(cnt, own, hal, attr_j, attr_i, tab_j, tab_i):
    return call(
        density_kernel,
        "density",
        (cnt, own, hal, attr_j, attr_i, tab_j, tab_i),
        (0,),
        (WIDE, COLS, ((NJ, 128), I32), ROW, lanes(4)),
        (
            pltpu.VMEM((1024, 8), F32),
            pltpu.VMEM((8, 1024), F32),
            pltpu.VMEM((NJ, 128), F32),
            pltpu.VMEM((NJ, 128), F32),
            pltpu.SMEM((NJ, 128), I32),
            pltpu.SemaphoreType.DMA,
            pltpu.VMEM((8, 4096), F32),
            pltpu.VMEM((1, 1024 + SB, 128), F32),
        ),
    )


def pressure(rho_row, held):
    padded = jnp.where(held, rho_row, 1.0)
    inverse = 1.0 / padded
    return 24.0 * (padded - 1.0) * inverse * inverse, 3.0 * inverse


def pressure_tables(cnt, rho, rho_h, tab_j, tab_i, mc, cc, stage):
    spread(rho, rho_h, stage, 1)
    row8 = iota((8, 128), 0)

    def table(got, held):
        coef, inv = pressure(got, held)
        return jnp.where(row8 == 0, coef, jnp.where(row8 == 1, inv, 0.0))

    def fill(m, _):
        idx, blk = entry(tab_j, m, NJ + m)
        put(mc, m, table(pick(stage, 0, 4, idx, blk), tab_j[pl.ds(NJ + m, 1), :] >= 0))
        return 0

    each_block(cnt, fill)
    for k in range(NI):
        idx, blk = entry(tab_i, k, NI + k)
        columns(cc, k, table(pick(stage, 0, 1, idx, blk), tab_i[NI + k : NI + k + 1, :] >= 0))


def force_kernel(cnt, win, rho, rho_h, own, mj, geo, tab_j, tab_i, mc, cc, new, cols, rows, stage, wide, sums):
    pressure_tables(cnt, rho, rho_h, tab_j, tab_i, mc, cc, stage)
    broadcast_columns(cnt, [(cc, 0, wide, 0)], sums, 4)

    def rows_at(m):
        return spot(mj, m), [row_of(mj, c, m) for c in (3, 4, 5)], row_of(mc, 0, m), row_of(mc, 1, m) * (1.0 / 6.0)

    def body(other, xi, yi, zi, bi, ci):
        spots, (vx, vy, vz), cj, pj = other
        dx, dy, dz, q = geometry(spots, xi, yi, zi, bi)
        q2 = q * q
        push = (ci + cj) * q2
        drag = q2 * q * pj
        return drag * vx - push * dx, drag * vy - push * dy, drag * vz - push * dz, drag

    pairs(cnt, win, rows_at, body, places((geo, 4), (wide, 1)), sums)


    def store(k, got):
        at = slice(128 * k, 128 * k + 128)
        v = [own[3 + c : 4 + c, at] for c in range(3)]
        v = [v[c] + (DT * MU) * (got[c : c + 1] - v[c] * got[3:4]) for c in range(3)]
        x = [own[c : c + 1, at] + DT * v[c] for c in range(3)]
        new[0:3, at] = jnp.concatenate(x, axis=0)
        new[3:6, at] = jnp.concatenate(v, axis=0)
        new[6:8, at] = own[6:8, at]

    sums_to_own(cnt, sums, 4, cols, rows, tab_i, store)


def force(cnt, win, rho, rho_h, own, mj, geo, tab_j, tab_i):
    return call(
        force_kernel,
        "force",
        (cnt, win, rho, rho_h, own, mj, geo, tab_j, tab_i),
        (0, 1),
        (WIDE, COLS, OWN),
        scratch(1, 4),
    )


def pressure_kernel(cnt, rho, rho_h, tab_j, tab_i, mc, cc, stage):
    pressure_tables(cnt, rho, rho_h, tab_j, tab_i, mc, cc, stage)


def pressure_only(cnt, rho, rho_h, tab_j, tab_i):
    return call(pressure_kernel, "pressure", (cnt, rho, rho_h, tab_j, tab_i), (0,), (WIDE, COLS), scratch(0, 0)[2:3])


def first_kernel(cnt, win, own, grad, grad_h, rho, mj, geo, mc, tab_j, tab_i, mg, ga, out, by_vel, gc, cols, rows, stage, wide, sums):
    spread(grad, grad_h, stage, 3)
    none = jnp.zeros((5, 128), F32)

    def fill(m, _):
        idx, blk = entry(tab_j, m, NJ + m)
        got = [pick(stage, c, 4, idx, blk) for c in range(3)]
        put(mg, m, jnp.concatenate(got + [none], axis=0))
        return 0

    each_block(cnt, fill)
    for k in range(NI):
        idx, blk = entry(tab_i, k, NI + k)
        got = [pick(stage, c, 1, idx, blk) for c in range(3)]
        columns(gc, k, jnp.concatenate(got + [none], axis=0))
    broadcast_columns(cnt, [(gc, c, ga, c) for c in range(3)], sums, 6)

    def rows_at(m):
        g = [row_of(mg, c, m) for c in range(3)]
        v = [row_of(mj, c, m) for c in (3, 4, 5)]
        return spot(mj, m), g, v[0] * g[0] + v[1] * g[1] + v[2] * g[2], row_of(mc, 1, m)

    def body(other, xi, yi, zi, bi, ax, ay, az):
        spots, (bx, by, bz), work, pj = other
        dx, dy, dz, q = geometry(spots, xi, yi, zi, bi)
        q2 = q * q
        q3 = q2 * q
        dh = dx * (ax - bx) + dy * (ay - by) + dz * (az - bz)
        return q2 * dh, q3 * work, q3 * pj, q3 * bx, q3 * by, q3 * bz

    pairs(cnt, win, rows_at, body, places((geo, 4), (ga, 3)), sums)

    def store(k, got):
        at = slice(128 * k, 128 * k + 128)
        held = live_of(tab_i, k)[0:1]
        p = jnp.where(held, rho[0:1, at], 1.0)
        inv = 1.0 / p
        inv2 = inv * inv
        by_coef = (-6.0 * MU) * got[0:1]
        drag = got[1:2] - (own[3:4, at] * got[3:4] + own[4:5, at] * got[4:5] + own[5:6, at] * got[5:6])
        by_pad = (0.5 * MU) * inv2 * drag
        g_rho = by_coef * (4.0 * inv2 - 8.0 * (p - 1.0) * inv2 * inv) + by_pad
        out[0:1, at] = jnp.where(held, 6.0 * g_rho, 0.0)
        by_vel[0:3, at] = (-0.5 * MU) * (grad[0:3, at] * (got[2:3] * (1.0 / 3.0)) - inv * got[3:6])
        by_vel[3:4, at] = jnp.zeros((1, 128), F32)

    sums_to_own(cnt, sums, 6, cols, rows, tab_i, store)


def first_sweep(*ins):
    return call(
        first_kernel,
        "adjoint1",
        ins,
        (0, 1),
        (WIDE, lanes(3), ROW, GRAD),
        (pltpu.VMEM((1024, 8), F32),) + scratch(1, 6),
    )


def second_kernel(final, cnt, win, part, part_h, by_vel, carry, mj, ic, geo, mc, cc, mg, ga, tab_j, tab_i, grad, new, mp, pc, cols, rows, stage, wide, sums):
    spread(part, part_h, stage, 1)

    def fill(m, _):
        idx, blk = entry(tab_j, m, NJ + m)
        put(mp, m, jnp.broadcast_to(pick(stage, 0, 4, idx, blk), (8, 128)))
        return 0

    each_block(cnt, fill)
    for k in range(NI):
        idx, blk = entry(tab_i, k, NI + k)
        columns(pc, k, jnp.broadcast_to(pick(stage, 0, 1, idx, blk), (8, 128)))
    taken = [(ic, 3), (ic, 4), (ic, 5), (cc, 0), (cc, 1), (pc, 0)]
    broadcast_columns(cnt, [(ref, c, wide, n) for n, (ref, c) in enumerate(taken)], sums, 3)

    def rows_at(m):
        v = [row_of(mj, c, m) for c in (3, 4, 5)]
        g = [row_of(mg, c, m) for c in range(3)]
        return spot(mj, m), v, g, row_of(mc, 0, m), row_of(mc, 1, m), row_of(mp, 0, m)

    def body(other, xi, yi, zi, bi, ax, ay, az, ux, uy, uz, ci, pi, ri):
        spots, (vx, vy, vz), (bx, by, bz), cj, pj, rj = other
        dx, dy, dz, q = geometry(spots, xi, yi, zi, bi)
        hx, hy, hz = ax - bx, ay - by, az - bz
        wx, wy, wz = vx - ux, vy - uy, vz - uz
        dh = dx * hx + dy * hy + dz * hz
        ua = wx * ax + wy * ay + wz * az
        ub = wx * bx + wy * by + wz * bz
        coef = ci + cj
        along = q * (q * (ua * pj - ub * pi + (ri + rj)) - 4.0 * coef * dh)
        across = coef * (q * q)
        return along * dx + across * hx, along * dy + across * hy, along * dz + across * hz

    pairs(cnt, win, rows_at, body, places((geo, 4), (ga, 3), (wide, 6)), sums)

    def store(k, got):
        at = slice(128 * k, 128 * k + 128)
        gp = carry[0:3, at] + MU * got[0:3]
        gv = carry[3:6, at] + by_vel[0:3, at]
        if not final:
            gv = gv + DT * gp
            held = live_of(tab_i, k)[0:3]
            grad[0:3, at] = jnp.where(held, DT * gv, 0.0)
            grad[3:4, at] = jnp.zeros((1, 128), F32)
        else:
            grad[:, at] = jnp.zeros((4, 128), F32)
        new[0:3, at] = gp
        new[3:6, at] = gv
        new[6:8, at] = jnp.zeros((2, 128), F32)

    sums_to_own(cnt, sums, 3, cols, rows, tab_i, store)


def second_sweep(final, *ins):
    return call(
        functools.partial(second_kernel, final),
        "adjoint2",
        ins,
        (0, 1),
        (GRAD, OWN),
        (pltpu.VMEM((8, 4096), F32), pltpu.VMEM((1024, 8), F32)) + scratch(6, 3),
    )


def attributes(half):
    far = jnp.where(half == 0, 4.0, -1.0)
    tiles = [(0.0, float(b)) for b in range(4)] + [(-1.0, float(b)) for b in range(4)]
    tiles += [(1.0, float(b)) for b in range(4)] + [(0.0, far), (-1.0, far), (1.0, far), (0.0, 0.0)]
    zero = jnp.zeros((16,), F32)
    a = jnp.array([t[0] for t in tiles], F32)
    b = jnp.stack([jnp.asarray(t[1], F32) for t in tiles])
    return jnp.repeat(jnp.stack([a, b, zero, zero, zero, zero, b, zero]), 256, axis=1)


def per_device(nx, ny, positions, velocities, occupancy, cot_positions, cot_velocities):
    ring = 2 * nx
    flat = lambda a: a.reshape(3, 1024)
    slots = lax.broadcasted_iota(I32, (2, 2, 256), 2)
    live = (slots < occupancy[:, :, None]).astype(F32).reshape(1, 1024)
    zero = jnp.zeros((1, 1024), F32)
    state = jnp.concatenate(
        [flat(positions), flat(velocities), live, zero, flat(cot_positions), flat(cot_velocities), zero, zero], axis=0
    )
    gy_odd = lax.axis_index("gy") % 2
    column, half = mesh_to_logical(lax.axis_index("gx"), lax.axis_index("gy"))
    col_odd = column % 2

    def mesh_id(column, half):
        x, y = logical_to_mesh(column, half)
        return x * ny + y

    same = [(x * ny + y, mesh_id(2 * x + y % 2, y // 2)) for x in range(nx) for y in range(ny)]
    cross = [(x * ny + y, mesh_id(2 * x + 1 - y % 2, y // 2)) for x in range(nx) for y in range(ny)]

    def swap(value, odd, first, second):
        low, high = value[:, :512], value[:, 512:]
        one = lax.ppermute(jnp.where(odd == 0, low, high), ("gx", "gy"), first)
        two = lax.ppermute(jnp.where(odd == 0, high, low), ("gx", "gy"), second)
        return one, two

    def join(one, two, odd):
        return jnp.concatenate([jnp.where(odd == 0, one, two), jnp.where(odd == 0, two, one)], axis=1)

    state = join(*swap(state, gy_odd, same, cross), col_odd)
    grad_vel = state[11:14] + DT * state[8:11]
    grad = DT * state[6:7] * grad_vel
    carry = jnp.concatenate([state[8:11], grad_vel, jnp.zeros((2, 1024), F32)], axis=0)
    own = state[0:8]
    start = jnp.concatenate([own, grad, jnp.zeros((5, 1024), F32)], axis=0)
    attr_j = attributes(half)
    attr_i = attr_j[:, :1024]

    hal16 = halo(start, ring, 1)
    hal = hal16[0:8]
    grad, grad_h = start[8:12], hal16[8:12]
    tab_j, tab_i, cnt = plan(own, hal)
    history = []
    for step in range(STEPS):
        if step:
            hal = halo(own, ring, 0)
        mj, ic, win, rho, geo = density(cnt, own, hal, attr_j, attr_i, tab_j, tab_i)
        rho_h = halo(rho, ring, 2)
        before = own
        if step + 1 < STEPS:
            mc, cc, own = force(cnt, win, rho, rho_h, own, mj, geo, tab_j, tab_i)
        else:
            mc, cc = pressure_only(cnt, rho, rho_h, tab_j, tab_i)
        history.append((win, rho, mj, ic, geo, mc, cc, before))
    for step in reversed(range(STEPS)):
        win, rho, mj, ic, geo, mc, cc, state_at = history[step]
        mg, ga, part, by_vel = first_sweep(cnt, win, state_at, grad, grad_h, rho, mj, geo, mc, tab_j, tab_i)
        part_h = halo(part, ring, 2)
        grad, carry = second_sweep(
            step == 0, cnt, win, part, part_h, by_vel, carry, mj, ic, geo, mc, cc, mg, ga, tab_j, tab_i
        )
        if step:
            grad_h = halo(grad, ring, 3)
    back = lambda moves: [(d, s) for s, d in moves]
    result = join(*swap(carry, col_odd, back(same), back(cross)), gy_odd)
    return result[0:3].reshape(positions.shape), result[3:6].reshape(positions.shape)


def solution(mesh):
    spec = P(None, "gx", "gy", None)
    return jax.shard_map(
        functools.partial(per_device, mesh.shape["gx"], mesh.shape["gy"]),
        mesh=mesh,
        in_specs=(spec, spec, P("gx", "gy"), spec, spec),
        out_specs=(spec, spec),
        check_vma=False,
    )
```

time: 303 us -> 224 us (0.74)
  the two profiles are of different devices: /device:TPU:58 before, /device:TPU:66 now
where the time goes in v1:
time: 224 us; the launch traced here: 227 us
  Pallas kernels  182 us (81%)
  starting transfers between devices  24.9 us (11%)
  waiting for transfers between devices  13.1 us (6%)
  local copies, waits for them, and re-layouts  5.4 us (2%)
    pallas_call x16, Pallas kernels, call(): pl.pallas_call(kernel, out_shape=tuple((jax.ShapeDtypeStruct(s, t) for s,...  104 us
    pallas_call x15, Pallas kernels, halo(): pl.pallas_call(functools.partial(halo_kernel, ring), out_shape=jax.ShapeD...  76 us
    ppermute x2, starting transfers between devices, swap(): two = lax.ppermute(jnp.where(odd == 0, high, low), ('gx', 'gy'), second)  20 us
    ppermute x2, waiting for transfers between devices, swap(): one = lax.ppermute(jnp.where(odd == 0, low, high), ('gx', 'gy'), first)  13.1 us
    ppermute x2, starting transfers between devices, swap(): one = lax.ppermute(jnp.where(odd == 0, low, high), ('gx', 'gy'), first)  4.92 us
  transfers between devices with their start and end apart: 4, of which 2 were waited for; matrix products, arithmetic and copies ran while one was open for 0% of the time, Pallas kernels for 0%

profile of v1, /device:TPU:66, one launch (start us, length us, event | category | flops | bytes accessed | tf_op | source)
XLA Modules:
  0.0 227.1 jit_solution(12361719992283066133)
XLA Ops:
  4.4 7.8 %collective-permute-start.1 = (f32[16,512]{1,0:T(8,128)S(1)}, f32[16,512]{1,0:T(8,128)S(1)}, u32[]{:S(2)}, u32[]{:S(2)}) collective-permute-start(f32[16,512]{1,0:T(8,128)S(1)} %get-tuple-element.121), channel_id=1, source_target_pairs={{0,32},{1,0},{2,33},{3,1},{4,34},{5,2},{6,35},{7,3},{8,6},{9,38},{... | collective-permute-start | bytes 98312 | tf_op jit(solution)/shard_map/ppermute | solution.py:657
  20.6 7.3 %halo16.1 = f32[16,3072]{1,0:T(8,128)S(1)} custom-call(f32[16,1024]{1,0:T(8,128)S(1)} %maximum_maximum_fusion.src), custom_call_target="tpu_custom_call" | custom-call | tf_op jit(solution)/shard_map/halo16/pallas_call | solution.py:79
  30.0 5.9 %density.4 = (f32[8,4096]{1,0:T(8,128)S(1)}, f32[1024,8]{1,0:T(8,128)S(1)}, s32[32,128]{1,0:T(8,128)S(1)}, f32[1,1024]{1,0:T(1,128)S(1)}, f32[4,1056,128]{2,1,0:T(8,128)S(1)}) custom-call(s32[1,128]{1,0:T(1,128)S(1)} %get-tuple-element.59.cnt, f32[8,1024]{1,0:T(8,128)S(1)} %fusion.own, f32[8,3072]{1,0:T(8,128)S(1)} %slice.50.hal, f32[8,4096]{1,0:T(8,128)S(1)} %bitcast.5, ...), custom_call_target="tpu_custom_call" | custom-call | tf_op jit(solution)/shard_map/density/pallas_call | solution.py:372
  39.8 5.9 %force.3 = (f32[8,4096]{1,0:T(8,128)S(1)}, f32[1024,8]{1,0:T(8,128)S(1)}, f32[8,1024]{1,0:T(8,128)S(1)}) custom-call(s32[1,128]{1,0:T(1,128)S(1)} %get-tuple-element.59.cnt, s32[32,128]{1,0:T(8,128)S(1)} %get-tuple-element.62.win, f32[1,1024]{1,0:T(1,128)S(1)} %get-tuple-element.63.src.rho, f32[1,3072]{1,0:T(1,128)S(1)} %halo1.8.rho_h, ...), custom_call_target="tpu_custom_call" | custom-call | tf_op jit(solution)/shard_map/force/pallas_call | solution.py:372
  50.1 5.9 %density.5 = (f32[8,4096]{1,0:T(8,128)S(1)}, f32[1024,8]{1,0:T(8,128)S(1)}, s32[32,128]{1,0:T(8,128)S(1)}, f32[1,1024]{1,0:T(1,128)S(1)}, f32[4,1056,128]{2,1,0:T(8,128)S(1)}) custom-call(s32[1,128]{1,0:T(1,128)S(1)} %get-tuple-element.59.cnt, f32[8,1024]{1,0:T(8,128)S(1)} %get-tuple-element.66.src.own, f32[8,3072]{1,0:T(8,128)S(1)} %halo8.3.hal, ...), custom_call_target="tpu_custom_call" | custom-call | tf_op jit(solution)/shard_map/density/pallas_call | solution.py:372
  60.0 5.9 %force.4 = (f32[8,4096]{1,0:T(8,128)S(1)}, f32[1024,8]{1,0:T(8,128)S(1)}, f32[8,1024]{1,0:T(8,128)S(1)}) custom-call(s32[1,128]{1,0:T(1,128)S(1)} %get-tuple-element.59.cnt, s32[32,128]{1,0:T(8,128)S(1)} %get-tuple-element.67.win, f32[1,1024]{1,0:T(1,128)S(1)} %get-tuple-element.68.src.rho, f32[1,3072]{1,0:T(1,128)S(1)} %halo1.9.rho_h, ...), custom_call_target="tpu_custom_call" | custom-call | tf_op jit(solution)/shard_map/force/pallas_call | solution.py:372
  70.2 6.0 %density.6 = (f32[8,4096]{1,0:T(8,128)S(1)}, f32[1024,8]{1,0:T(8,128)S(1)}, s32[32,128]{1,0:T(8,128)S(1)}, f32[1,1024]{1,0:T(1,128)S(1)}, f32[4,1056,128]{2,1,0:T(8,128)S(1)}) custom-call(s32[1,128]{1,0:T(1,128)S(1)} %get-tuple-element.59.cnt, f32[8,1024]{1,0:T(8,128)S(1)} %get-tuple-element.71.src.own, f32[8,3072]{1,0:T(8,128)S(1)} %halo8.4.hal, ...), custom_call_target="tpu_custom_call" | custom-call | tf_op jit(solution)/shard_map/density/pallas_call | solution.py:372
  80.1 5.9 %force.5 = (f32[8,4096]{1,0:T(8,128)S(1)}, f32[1024,8]{1,0:T(8,128)S(1)}, f32[8,1024]{1,0:T(8,128)S(1)}) custom-call(s32[1,128]{1,0:T(1,128)S(1)} %get-tuple-element.59.cnt, s32[32,128]{1,0:T(8,128)S(1)} %get-tuple-element.72.win, f32[1,1024]{1,0:T(1,128)S(1)} %get-tuple-element.73.src.rho, f32[1,3072]{1,0:T(1,128)S(1)} %halo1.10.rho_h, ...), custom_call_target="tpu_custom_call" | custom-call | tf_op jit(solution)/shard_map/force/pallas_call | solution.py:372
  91.1 6.0 %density.7 = (f32[8,4096]{1,0:T(8,128)S(1)}, f32[1024,8]{1,0:T(8,128)S(1)}, s32[32,128]{1,0:T(8,128)S(1)}, f32[1,1024]{1,0:T(1,128)S(1)}, f32[4,1056,128]{2,1,0:T(8,128)S(1)}) custom-call(s32[1,128]{1,0:T(1,128)S(1)} %get-tuple-element.59.cnt, f32[8,1024]{1,0:T(8,128)S(1)} %get-tuple-element.76.src.own, f32[8,3072]{1,0:T(8,128)S(1)} %halo8.5.hal, ...), custom_call_target="tpu_custom_call" | custom-call | tf_op jit(solution)/shard_map/density/pallas_call | solution.py:372
  97.1 5.2 %halo1.11.rho_h = f32[1,3072]{1,0:T(1,128)S(1)} custom-call(f32[1,1024]{1,0:T(1,128)S(1)} %get-tuple-element.78.src.rho), custom_call_target="tpu_custom_call" | custom-call | tf_op jit(solution)/shard_map/halo1/pallas_call | solution.py:79
  103.7 6.9 %adjoint1.4 = (f32[8,4096]{1,0:T(8,128)S(1)}, f32[3,1056,128]{2,1,0:T(8,128)S(1)}, f32[1,1024]{1,0:T(1,128)S(1)}, f32[4,1024]{1,0:T(4,128)S(1)}) custom-call(s32[1,128]{1,0:T(1,128)S(1)} %get-tuple-element.59.cnt, s32[32,128]{1,0:T(8,128)S(1)} %get-tuple-element.77.win, f32[8,1024]{1,0:T(8,128)S(1)} %get-tuple-element.76.src.own, ...), custom_call_target="tpu_custom_call" | custom-call | tf_op jit(solution)/shard_map/adjoint1/pallas_call | solution.py:372
  110.6 5.6 %halo1.12.part_h = f32[1,3072]{1,0:T(1,128)S(1)} custom-call(f32[1,1024]{1,0:T(1,128)S(1)} %get-tuple-element.82.src.part), custom_call_target="tpu_custom_call" | custom-call | tf_op jit(solution)/shard_map/halo1/pallas_call | solution.py:79
  116.2 8.4 %adjoint2.4 = (f32[4,1024]{1,0:T(4,128)S(1)}, f32[8,1024]{1,0:T(8,128)S(1)}) custom-call(s32[1,128]{1,0:T(1,128)S(1)} %get-tuple-element.59.cnt, s32[32,128]{1,0:T(8,128)S(1)} %get-tuple-element.77.win, f32[1,1024]{1,0:T(1,128)S(1)} %get-tuple-element.82.src.part, f32[1,3072]{1,0:T(1,128)S(1)} %halo1.12.part_h, f32[4,1024]{1,0:T(4,128)S(1)} %get-tuple-element.83.by_vel, ...), custom_call_target="tpu_custom_call" | custom-call | tf_op jit(solution)/shard_map/adjoint2/pallas_call | solution.py:372
  124.7 5.9 %halo4.3.grad_h = f32[4,3072]{1,0:T(4,128)S(1)} custom-call(f32[4,1024]{1,0:T(4,128)S(1)} %get-tuple-element.88.src.grad), custom_call_target="tpu_custom_call" | custom-call | tf_op jit(solution)/shard_map/halo4/pallas_call | solution.py:79
  130.6 6.8 %adjoint1.5 = (f32[8,4096]{1,0:T(8,128)S(1)}, f32[3,1056,128]{2,1,0:T(8,128)S(1)}, f32[1,1024]{1,0:T(1,128)S(1)}, f32[4,1024]{1,0:T(4,128)S(1)}) custom-call(s32[1,128]{1,0:T(1,128)S(1)} %get-tuple-element.59.cnt, s32[32,128]{1,0:T(8,128)S(1)} %get-tuple-element.72.win, f32[8,1024]{1,0:T(8,128)S(1)} %get-tuple-element.71.src.own, ...), custom_call_target="tpu_custom_call" | custom-call | tf_op jit(solution)/shard_map/adjoint1/pallas_call | solution.py:372
  141.7 8.4 %adjoint2.5 = (f32[4,1024]{1,0:T(4,128)S(1)}, f32[8,1024]{1,0:T(8,128)S(1)}) custom-call(s32[1,128]{1,0:T(1,128)S(1)} %get-tuple-element.59.cnt, s32[32,128]{1,0:T(8,128)S(1)} %get-tuple-element.72.win, f32[1,1024]{1,0:T(1,128)S(1)} %get-tuple-element.90.src.part, f32[1,3072]{1,0:T(1,128)S(1)} %halo1.13.part_h, f32[4,1024]{1,0:T(4,128)S(1)} %get-tuple-element.91.by_vel, ...), custom_call_target="tpu_custom_call" | custom-call | tf_op jit(solution)/shard_map/adjoint2/pallas_call | solution.py:372
  150.1 6.2 %halo4.4.grad_h = f32[4,3072]{1,0:T(4,128)S(1)} custom-call(f32[4,1024]{1,0:T(4,128)S(1)} %get-tuple-element.97.src.grad), custom_call_target="tpu_custom_call" | custom-call | tf_op jit(solution)/shard_map/halo4/pallas_call | solution.py:79
  156.3 6.7 %adjoint1.6 = (f32[8,4096]{1,0:T(8,128)S(1)}, f32[3,1056,128]{2,1,0:T(8,128)S(1)}, f32[1,1024]{1,0:T(1,128)S(1)}, f32[4,1024]{1,0:T(4,128)S(1)}) custom-call(s32[1,128]{1,0:T(1,128)S(1)} %get-tuple-element.59.cnt, s32[32,128]{1,0:T(8,128)S(1)} %get-tuple-element.67.win, f32[8,1024]{1,0:T(8,128)S(1)} %get-tuple-element.66.src.own, ...), custom_call_target="tpu_custom_call" | custom-call | tf_op jit(solution)/shard_map/adjoint1/pallas_call | solution.py:372
  167.8 8.3 %adjoint2.6 = (f32[4,1024]{1,0:T(4,128)S(1)}, f32[8,1024]{1,0:T(8,128)S(1)}) custom-call(s32[1,128]{1,0:T(1,128)S(1)} %get-tuple-element.59.cnt, s32[32,128]{1,0:T(8,128)S(1)} %get-tuple-element.67.win, f32[1,1024]{1,0:T(1,128)S(1)} %get-tuple-element.99.src.part, f32[1,3072]{1,0:T(1,128)S(1)} %halo1.14.part_h, f32[4,1024]{1,0:T(4,128)S(1)} %get-tuple-element.100.by_vel, ...), custom_call_target="tpu_custom_call" | custom-call | tf_op jit(solution)/shard_map/adjoint2/pallas_call | solution.py:372
  176.1 6.4 %halo4.5.grad_h = f32[4,3072]{1,0:T(4,128)S(1)} custom-call(f32[4,1024]{1,0:T(4,128)S(1)} %get-tuple-element.106.src.grad), custom_call_target="tpu_custom_call" | custom-call | tf_op jit(solution)/shard_map/halo4/pallas_call | solution.py:79
  182.5 6.7 %adjoint1.7 = (f32[8,4096]{1,0:T(8,128)S(1)}, f32[3,1056,128]{2,1,0:T(8,128)S(1)}, f32[1,1024]{1,0:T(1,128)S(1)}, f32[4,1024]{1,0:T(4,128)S(1)}) custom-call(s32[1,128]{1,0:T(1,128)S(1)} %get-tuple-element.59.cnt, s32[32,128]{1,0:T(8,128)S(1)} %get-tuple-element.62.win, f32[8,1024]{1,0:T(8,128)S(1)} %fusion.own, f32[4,1024]{1,0:T(4,128)S(1)} %get-tuple-element.106.src.grad, ...), custom_call_target="tpu_custom_call" | custom-call | tf_op jit(solution)/shard_map/adjoint1/pallas_call | solution.py:372
  193.8 8.7 %adjoint2.7 = (f32[4,1024]{1,0:T(4,128)}, f32[8,1024]{1,0:T(8,128)S(1)}) custom-call(s32[1,128]{1,0:T(1,128)S(1)} %get-tuple-element.59.cnt, s32[32,128]{1,0:T(8,128)S(1)} %get-tuple-element.62.win, f32[1,1024]{1,0:T(1,128)S(1)} %get-tuple-element.108.src.part, f32[1,3072]{1,0:T(1,128)S(1)} %halo1.15.part_h, f32[4,1024]{1,0:T(4,128)S(1)} %get-tuple-element.109.by_vel, ...), custom_call_target="tpu_custom_call" | custom-call | tf_op jit(solution)/shard_map/adjoint2/pallas_call | solution.py:372
  202.5 12.2 %collective-permute-start.3 = (f32[8,512]{1,0:T(8,128)S(1)}, f32[8,512]{1,0:T(8,128)S(1)}, u32[]{:S(2)}, u32[]{:S(2)}) collective-permute-start(f32[8,512]{1,0:T(8,128)S(1)} %get-tuple-element.127), channel_id=1, source_target_pairs={{32,0},{0,1},{33,2},{1,3},{34,4},{2,5},{35,6},{3,7},{6,8},{38,9},{... | collective-permute-start | bytes 49160 | tf_op jit(solution)/shard_map/ppermute | solution.py:657
  216.7 9.1 %collective-permute-done.2 = f32[8,512]{1,0:T(8,128)S(1)} collective-permute-done((f32[8,512]{1,0:T(8,128)S(1)}, f32[8,512]{1,0:T(8,128)S(1)}, u32[]{:S(2)}, u32[]{:S(2)}) %collective-permute-start.2) | collective-permute-done | bytes 16416 | tf_op jit(solution)/shard_map/ppermute | solution.py:656
  (49 shorter events, 57.9 us)
Async XLA Ops:
  4.4 12.1 %collective-permute-start.1 = (f32[16,512]{1,0:T(8,128)S(1)}, f32[16,512]{1,0:T(8,128)S(1)}, u32[]{:S(2)}, u32[]{:S(2)}) collective-permute-start(f32[16,512]{1,0:T(8,128)S(1)} %get-tuple-element.121), channel_id=1, source_target_pairs={{0,32},{1,0},{2,33},{3,1},{4,34},{5,2},{6,35},{7,3},{8,6},{9,38},{... | collective-permute-start | bytes 98312 | tf_op jit(solution)/shard_map/ppermute | solution.py:657
  12.2 8.2 %collective-permute-start = (f32[16,512]{1,0:T(8,128)S(1)}, f32[16,512]{1,0:T(8,128)S(1)}, u32[]{:S(2)}, u32[]{:S(2)}) collective-permute-start(f32[16,512]{1,0:T(8,128)S(1)} %get-tuple-element.122), channel_id=1, source_target_pairs={{0,0},{1,32},{2,1},{3,33},{4,2},{5,34},{6,3},{7,35},{8,38},{9,6},{... | collective-permute-start | bytes 98312 | tf_op jit(solution)/shard_map/ppermute | solution.py:656
  202.5 14.2 %collective-permute-start.3 = (f32[8,512]{1,0:T(8,128)S(1)}, f32[8,512]{1,0:T(8,128)S(1)}, u32[]{:S(2)}, u32[]{:S(2)}) collective-permute-start(f32[8,512]{1,0:T(8,128)S(1)} %get-tuple-element.127), channel_id=1, source_target_pairs={{32,0},{0,1},{33,2},{1,3},{34,4},{2,5},{35,6},{3,7},{6,8},{38,9},{... | collective-permute-start | bytes 49160 | tf_op jit(solution)/shard_map/ppermute | solution.py:657
  214.8 11.0 %collective-permute-start.2 = (f32[8,512]{1,0:T(8,128)S(1)}, f32[8,512]{1,0:T(8,128)S(1)}, u32[]{:S(2)}, u32[]{:S(2)}) collective-permute-start(f32[8,512]{1,0:T(8,128)S(1)} %get-tuple-element.128), channel_id=1, source_target_pairs={{0,0},{32,1},{1,2},{33,3},{2,4},{34,5},{3,6},{35,7},{38,8},{6,9},{... | collective-permute-start | bytes 49160 | tf_op jit(solution)/shard_map/ppermute | solution.py:656

commit v2 on v1

--- a/solution.py
+++ b/solution.py
@@ -2,6 +2,7 @@
 
 import jax
 import jax.numpy as jnp
+import numpy as np
 from jax import lax
 from jax.experimental import pallas as pl
 from jax.experimental.pallas import tpu as pltpu
@@ -15,7 +16,7 @@
 I32 = jnp.int32
 NJ, NI = 32, 8
 NK = 30
-SB = 32
+PAD = 64
 NS = 128
 REACH = 1.0001
 
@@ -157,7 +158,7 @@
     ni = jnp.sum(total_i, axis=0, keepdims=True)
     at = iota((1, 128), 1)
     blocks_j = (nj + 127.0).astype(I32) >> 7
-    groups_i = (ni + (SB - 1.0)).astype(I32) >> 5
+    groups_i = (ni + 31.0).astype(I32) >> 5
     cnt[...] = jnp.where(at == 0, blocks_j, groups_i)
 
 
@@ -217,7 +218,7 @@
             fill(together * b + n, 0)
         return 0
 
-    lax.fori_loop(0, (cnt[0, 0] + together - 1) // together, several, 0)
+    lax.fori_loop(0, (cnt[0, 0] + together - 1) >> (together.bit_length() - 1), several, 0)
 
 
 def block(ref, m):
@@ -261,19 +262,19 @@
     lax.fori_loop(0, (cnt[0, 1] + 3) >> 2, one, 0)
 
 
-def pairs(cnt, win, rows, body, mine, sums):
+def pairs(cnt, win, rows, body, mine, sums, size=32):
     def each(m, _):
         picked = rows(m)
         first = win[m, 0]
 
         def chunk(n, _):
-            at = pl.multiple_of((first + 4 * n) * 8, 8)
-            terms = body(picked, *[wide[c, pl.ds(at, SB), :] for wide, c in mine])
+            at = pl.multiple_of((first + (size // 8) * n) * 8, 8)
+            terms = body(picked, *[wide[c, pl.ds(at, size), :] for wide, c in mine])
             for c, term in enumerate(terms):
-                sums[c, pl.ds(at, SB), :] += term
+                sums[c, pl.ds(at, size), :] += term
             return 0
 
-        lax.fori_loop(0, win[m, 1], chunk, 0)
+        lax.fori_loop(0, (win[m, 1] + (size - 1)) >> (size.bit_length() - 1), chunk, 0)
         return 0
 
     lax.fori_loop(0, cnt[0, 0], each, 0)
@@ -292,7 +293,7 @@
 
 
 def geometry(spots, xi, yi, zi, bi):
-    xj, yj, zj, bj = [jnp.broadcast_to(r, (SB, 128)) for r in spots]
+    xj, yj, zj, bj = [jnp.broadcast_to(r, xi.shape) for r in spots]
     dx, dy, dz, db = xj - xi, yj - yi, zj - zi, bj - bi
     top = jnp.minimum(2.0 - db * db, 1.0)
     q = jnp.maximum(top - (dx * dx + dy * dy + dz * dz), 0.0)
@@ -347,7 +348,7 @@
         last = jnp.maximum(last, jnp.where(meets, at + 1, 0))
     first = jnp.min(first.astype(F32), axis=1, keepdims=True).astype(I32) >> 3
     last = jnp.max(last.astype(F32), axis=1, keepdims=True).astype(I32)
-    chunks = jnp.maximum(last - 8 * first + (SB - 1), 0) >> 5
+    chunks = jnp.maximum(last - 8 * first, 0)
     windows = jnp.where(iota((NJ, 128), 1) == 0, first, chunks)
     win[...] = windows
     copy = pltpu.make_async_copy(win, win_s, sem)
@@ -359,7 +360,7 @@
         _, _, _, q = geometry(spots, *mine)
         return (q * q * q,)
 
-    pairs(cnt, win_s, lambda m: spot(mj, m), body, places((geo, 4)), sums)
+    pairs(cnt, win_s, lambda m: spot(mj, m), body, places((geo, 4)), sums, 64)
 
     def store(k, got):
         rho[:, 128 * k : 128 * k + 128] = MU * got[0:1]
@@ -385,8 +386,8 @@
         pltpu.VMEM((1024, 8), F32),
         pltpu.VMEM((8, 1024), F32),
         pltpu.VMEM((8 * NJ, 128), F32),
-        pltpu.VMEM((n_in, 1024 + SB, 128), F32),
-        pltpu.VMEM((n_out, 1024 + SB, 128), F32),
+        pltpu.VMEM((n_in, 1024 + PAD, 128), F32),
+        pltpu.VMEM((n_out, 1024 + PAD, 128), F32),
     )
 
 
@@ -396,7 +397,7 @@
 
 
 def lanes(n):
-    return ((n, 1024 + SB, 128), F32)
+    return ((n, 1024 + PAD, 128), F32)
 
 
 GRAD = ((4, 1024), F32)
@@ -418,7 +419,7 @@
             pltpu.SMEM((NJ, 128), I32),
             pltpu.SemaphoreType.DMA,
             pltpu.VMEM((8, 4096), F32),
-            pltpu.VMEM((1, 1024 + SB, 128), F32),
+            pltpu.VMEM((1, 1024 + PAD, 128), F32),
         ),
     )
 
@@ -463,7 +464,7 @@
         drag = q2 * q * pj
         return drag * vx - push * dx, drag * vy - push * dy, drag * vz - push * dz, drag
 
-    pairs(cnt, win, rows_at, body, places((geo, 4), (wide, 1)), sums)
+    pairs(cnt, win, rows_at, body, places((geo, 4), (wide, 1)), sums, 32)
 
 
     def store(k, got):
@@ -489,14 +490,6 @@
     )
 
 
-def pressure_kernel(cnt, rho, rho_h, tab_j, tab_i, mc, cc, stage):
-    pressure_tables(cnt, rho, rho_h, tab_j, tab_i, mc, cc, stage)
-
-
-def pressure_only(cnt, rho, rho_h, tab_j, tab_i):
-    return call(pressure_kernel, "pressure", (cnt, rho, rho_h, tab_j, tab_i), (0,), (WIDE, COLS), scratch(0, 0)[2:3])
-
-
 def first_kernel(cnt, win, own, grad, grad_h, rho, mj, geo, mc, tab_j, tab_i, mg, ga, out, by_vel, gc, cols, rows, stage, wide, sums):
     spread(grad, grad_h, stage, 3)
     none = jnp.zeros((5, 128), F32)
@@ -527,7 +520,7 @@
         dh = dx * (ax - bx) + dy * (ay - by) + dz * (az - bz)
         return q2 * dh, q3 * work, q3 * pj, q3 * bx, q3 * by, q3 * bz
 
-    pairs(cnt, win, rows_at, body, places((geo, 4), (ga, 3)), sums)
+    pairs(cnt, win, rows_at, body, places((geo, 4), (ga, 3)), sums, 32)
 
     def store(k, got):
         at = slice(128 * k, 128 * k + 128)
@@ -546,13 +539,20 @@
     sums_to_own(cnt, sums, 6, cols, rows, tab_i, store)
 
 
-def first_sweep(*ins):
+def first_with_pressure(cnt, win, rho_h, own, grad, grad_h, rho, mj, geo, tab_j, tab_i, mg, ga, out, by_vel, mc, cc, gc, cols, rows, stage, wide, sums):
+    pressure_tables(cnt, rho, rho_h, tab_j, tab_i, mc, cc, stage)
+    first_kernel(
+        cnt, win, own, grad, grad_h, rho, mj, geo, mc, tab_j, tab_i, mg, ga, out, by_vel, gc, cols, rows, stage, wide, sums
+    )
+
+
+def first_sweep(kernel, *ins):
     return call(
-        first_kernel,
+        kernel,
         "adjoint1",
         ins,
         (0, 1),
-        (WIDE, lanes(3), ROW, GRAD),
+        (WIDE, lanes(3), ROW, GRAD) + ((WIDE, COLS) if kernel is first_with_pressure else ()),
         (pltpu.VMEM((1024, 8), F32),) + scratch(1, 6),
     )
 
@@ -621,25 +621,21 @@
     )
 
 
-def attributes(half):
-    far = jnp.where(half == 0, 4.0, -1.0)
-    tiles = [(0.0, float(b)) for b in range(4)] + [(-1.0, float(b)) for b in range(4)]
-    tiles += [(1.0, float(b)) for b in range(4)] + [(0.0, far), (-1.0, far), (1.0, far), (0.0, 0.0)]
-    zero = jnp.zeros((16,), F32)
-    a = jnp.array([t[0] for t in tiles], F32)
-    b = jnp.stack([jnp.asarray(t[1], F32) for t in tiles])
-    return jnp.repeat(jnp.stack([a, b, zero, zero, zero, zero, b, zero]), 256, axis=1)
+def attributes(far):
+    tiles = [(a, float(b)) for a in (0.0, -1.0, 1.0) for b in range(4)]
+    tiles += [(0.0, far), (-1.0, far), (1.0, far), (0.0, 0.0)]
+    table = np.array([[a, b, 0, 0, 0, 0, b, 0] for a, b in tiles], np.float32).T
+    return jnp.asarray(np.repeat(table, 256, axis=1))
 
 
 def per_device(nx, ny, positions, velocities, occupancy, cot_positions, cot_velocities):
     ring = 2 * nx
-    flat = lambda a: a.reshape(3, 1024)
-    slots = lax.broadcasted_iota(I32, (2, 2, 256), 2)
-    live = (slots < occupancy[:, :, None]).astype(F32).reshape(1, 1024)
-    zero = jnp.zeros((1, 1024), F32)
+    slots = lax.broadcasted_iota(I32, (1, 2, 2, 256), 3)
+    live = (slots < occupancy[None, :, :, None]).astype(F32)
+    zero = jnp.zeros((1, 2, 2, 256), F32)
     state = jnp.concatenate(
-        [flat(positions), flat(velocities), live, zero, flat(cot_positions), flat(cot_velocities), zero, zero], axis=0
-    )
+        [positions, velocities, live, zero, cot_positions, cot_velocities, zero, zero], axis=0
+    ).reshape(16, 1024)
     gy_odd = lax.axis_index("gy") % 2
     column, half = mesh_to_logical(lax.axis_index("gx"), lax.axis_index("gy"))
     col_odd = column % 2
@@ -666,7 +662,7 @@
     carry = jnp.concatenate([state[8:11], grad_vel, jnp.zeros((2, 1024), F32)], axis=0)
     own = state[0:8]
     start = jnp.concatenate([own, grad, jnp.zeros((5, 1024), F32)], axis=0)
-    attr_j = attributes(half)
+    attr_j = jnp.where(half == 0, attributes(4.0), attributes(-1.0))
     attr_i = attr_j[:, :1024]
 
     hal16 = halo(start, ring, 1)
@@ -683,11 +679,18 @@
         if step + 1 < STEPS:
             mc, cc, own = force(cnt, win, rho, rho_h, own, mj, geo, tab_j, tab_i)
         else:
-            mc, cc = pressure_only(cnt, rho, rho_h, tab_j, tab_i)
+            mc = cc = None
         history.append((win, rho, mj, ic, geo, mc, cc, before))
     for step in reversed(range(STEPS)):
         win, rho, mj, ic, geo, mc, cc, state_at = history[step]
-        mg, ga, part, by_vel = first_sweep(cnt, win, state_at, grad, grad_h, rho, mj, geo, mc, tab_j, tab_i)
+        if mc is None:
+            mg, ga, part, by_vel, mc, cc = first_sweep(
+                first_with_pressure, cnt, win, rho_h, state_at, grad, grad_h, rho, mj, geo, tab_j, tab_i
+            )
+        else:
+            mg, ga, part, by_vel = first_sweep(
+                first_kernel, cnt, win, state_at, grad, grad_h, rho, mj, geo, mc, tab_j, tab_i
+            )
         part_h = halo(part, ring, 2)
         grad, carry = second_sweep(
             step == 0, cnt, win, part, part_h, by_vel, carry, mj, ic, geo, mc, cc, mg, ga, tab_j, tab_i
@@ -696,7 +699,8 @@
             grad_h = halo(grad, ring, 3)
     back = lambda moves: [(d, s) for s, d in moves]
     result = join(*swap(carry, col_odd, back(same), back(cross)), gy_odd)
-    return result[0:3].reshape(positions.shape), result[3:6].reshape(positions.shape)
+    result = result[0:6].reshape((6,) + positions.shape[1:])
+    return result[0:3], result[3:6]
 
 
 def solution(mesh):

time: 224 us -> 226 us (level)
  the two profiles are of different devices: /device:TPU:66 before, /device:TPU:89 now
where the time goes in v2:
time: 226 us; the launch traced here: 222 us
  Pallas kernels  179 us (79%)
  starting transfers between devices  24 us (11%)
  waiting for transfers between devices  12 us (5%)
  local copies, waits for them, and re-layouts  4.35 us (2%)
    pallas_call x15, Pallas kernels, halo(): pl.pallas_call(functools.partial(halo_kernel, ring), out_shape=jax.ShapeD...  104 us
    pallas_call x15, Pallas kernels, call(): pl.pallas_call(kernel, out_shape=tuple((jax.ShapeDtypeStruct(s, t) for s,...  73.5 us
    ppermute x2, starting transfers between devices, swap(): two = lax.ppermute(jnp.where(odd == 0, high, low), ('gx', 'gy'), second)  19.1 us
    ppermute x2, waiting for transfers between devices, swap(): one = lax.ppermute(jnp.where(odd == 0, low, high), ('gx', 'gy'), first)  12 us
    ppermute x2, starting transfers between devices, swap(): one = lax.ppermute(jnp.where(odd == 0, low, high), ('gx', 'gy'), first)  4.99 us
  transfers between devices with their start and end apart: 4, of which 2 were waited for; matrix products, arithmetic and copies ran while one was open for 0% of the time, Pallas kernels for 0%

profile of v2, /device:TPU:89, one launch (start us, length us, event | category | flops | bytes accessed | tf_op | source)
XLA Modules:
  0.0 222.5 jit_solution(17596155278410638780)
XLA Ops:
  4.4 9.8 %collective-permute-start.1 = (f32[16,512]{1,0:T(8,128)S(1)}, f32[16,512]{1,0:T(8,128)S(1)}, u32[]{:S(2)}, u32[]{:S(2)}) collective-permute-start(f32[16,512]{1,0:T(8,128)S(1)} %get-tuple-element.121), channel_id=1, source_target_pairs={{0,32},{1,0},{2,33},{3,1},{4,34},{5,2},{6,35},{7,3},{8,6},{9,38},{... | collective-permute-start | bytes 98312 | tf_op jit(solution)/shard_map/ppermute | solution.py:653
  21.1 6.4 %halo16.1 = f32[16,3072]{1,0:T(8,128)S(1)} custom-call(f32[16,1024]{1,0:T(8,128)S(1)} %maximum_maximum_fusion.src), custom_call_target="tpu_custom_call" | custom-call | tf_op jit(solution)/shard_map/halo16/pallas_call | solution.py:80
  34.1 5.5 %halo1.8.rho_h = f32[1,3072]{1,0:T(1,128)S(1)} custom-call(f32[1,1024]{1,0:T(1,128)S(1)} %get-tuple-element.63.src.rho), custom_call_target="tpu_custom_call" | custom-call | tf_op jit(solution)/shard_map/halo1/pallas_call | solution.py:80
  43.7 5.8 %halo8.3.hal = f32[8,3072]{1,0:T(8,128)S(1)} custom-call(f32[8,1024]{1,0:T(8,128)S(1)} %get-tuple-element.66.src.own), custom_call_target="tpu_custom_call" | custom-call | tf_op jit(solution)/shard_map/halo8/pallas_call | solution.py:80
  54.2 5.7 %halo1.9.rho_h = f32[1,3072]{1,0:T(1,128)S(1)} custom-call(f32[1,1024]{1,0:T(1,128)S(1)} %get-tuple-element.68.src.rho), custom_call_target="tpu_custom_call" | custom-call | tf_op jit(solution)/shard_map/halo1/pallas_call | solution.py:80
  64.0 6.1 %halo8.4.hal = f32[8,3072]{1,0:T(8,128)S(1)} custom-call(f32[8,1024]{1,0:T(8,128)S(1)} %get-tuple-element.71.src.own), custom_call_target="tpu_custom_call" | custom-call | tf_op jit(solution)/shard_map/halo8/pallas_call | solution.py:80
  74.7 5.8 %halo1.10.rho_h = f32[1,3072]{1,0:T(1,128)S(1)} custom-call(f32[1,1024]{1,0:T(1,128)S(1)} %get-tuple-element.73.src.rho), custom_call_target="tpu_custom_call" | custom-call | tf_op jit(solution)/shard_map/halo1/pallas_call | solution.py:80
  84.7 7.3 %halo8.5.hal = f32[8,3072]{1,0:T(8,128)S(1)} custom-call(f32[8,1024]{1,0:T(8,128)S(1)} %get-tuple-element.76.src.own), custom_call_target="tpu_custom_call" | custom-call | tf_op jit(solution)/shard_map/halo8/pallas_call | solution.py:80
  96.6 6.4 %halo1.11.rho_h = f32[1,3072]{1,0:T(1,128)S(1)} custom-call(f32[1,1024]{1,0:T(1,128)S(1)} %get-tuple-element.78.src.rho), custom_call_target="tpu_custom_call" | custom-call | tf_op jit(solution)/shard_map/halo1/pallas_call | solution.py:80
  103.0 5.7 %adjoint1.4 = (f32[8,4096]{1,0:T(8,128)S(1)}, f32[3,1088,128]{2,1,0:T(8,128)S(1)}, f32[1,1024]{1,0:T(1,128)S(1)}, f32[4,1024]{1,0:T(4,128)S(1)}, f32[8,4096]{1,0:T(8,128)S(1)}, /*index=5*/f32[1024,8]{1,0:T(8,128)S(1)}) custom-call(s32[1,128]{1,0:T(1,128)S(1)} %get-tuple-element.59.cnt, s32[32,128]{1,0:T(8,128)S(1)} %get-tuple-element.77.win, ...), custom_call_target="tpu_custom_call" | custom-call | tf_op jit(solution)/shard_map/adjoint1/pallas_call | solution.py:373
  108.7 8.3 %halo1.12.part_h = f32[1,3072]{1,0:T(1,128)S(1)} custom-call(f32[1,1024]{1,0:T(1,128)S(1)} %get-tuple-element.81.src.part), custom_call_target="tpu_custom_call" | custom-call | tf_op jit(solution)/shard_map/halo1/pallas_call | solution.py:80
  117.0 5.7 %adjoint2.4 = (f32[4,1024]{1,0:T(4,128)S(1)}, f32[8,1024]{1,0:T(8,128)S(1)}) custom-call(s32[1,128]{1,0:T(1,128)S(1)} %get-tuple-element.59.cnt, s32[32,128]{1,0:T(8,128)S(1)} %get-tuple-element.77.win, f32[1,1024]{1,0:T(1,128)S(1)} %get-tuple-element.81.src.part, f32[1,3072]{1,0:T(1,128)S(1)} %halo1.12.part_h, f32[4,1024]{1,0:T(4,128)S(1)} %get-tuple-element.82.by_vel, ...), custom_call_target="tpu_custom_call" | custom-call | tf_op jit(solution)/shard_map/adjoint2/pallas_call | solution.py:373
  122.7 7.9 %halo4.3.grad_h = f32[4,3072]{1,0:T(4,128)S(1)} custom-call(f32[4,1024]{1,0:T(4,128)S(1)} %get-tuple-element.88.src.grad), custom_call_target="tpu_custom_call" | custom-call | tf_op jit(solution)/shard_map/halo4/pallas_call | solution.py:80
  130.6 4.8 %adjoint1.5 = (f32[8,4096]{1,0:T(8,128)S(1)}, f32[3,1088,128]{2,1,0:T(8,128)S(1)}, f32[1,1024]{1,0:T(1,128)S(1)}, f32[4,1024]{1,0:T(4,128)S(1)}) custom-call(s32[1,128]{1,0:T(1,128)S(1)} %get-tuple-element.59.cnt, s32[32,128]{1,0:T(8,128)S(1)} %get-tuple-element.72.win, f32[8,1024]{1,0:T(8,128)S(1)} %get-tuple-element.71.src.own, ...), custom_call_target="tpu_custom_call" | custom-call | tf_op jit(solution)/shard_map/adjoint1/pallas_call | solution.py:373
  135.3 7.5 %halo1.13.part_h = f32[1,3072]{1,0:T(1,128)S(1)} custom-call(f32[1,1024]{1,0:T(1,128)S(1)} %get-tuple-element.90.src.part), custom_call_target="tpu_custom_call" | custom-call | tf_op jit(solution)/shard_map/halo1/pallas_call | solution.py:80
  142.8 5.7 %adjoint2.5 = (f32[4,1024]{1,0:T(4,128)S(1)}, f32[8,1024]{1,0:T(8,128)S(1)}) custom-call(s32[1,128]{1,0:T(1,128)S(1)} %get-tuple-element.59.cnt, s32[32,128]{1,0:T(8,128)S(1)} %get-tuple-element.72.win, f32[1,1024]{1,0:T(1,128)S(1)} %get-tuple-element.90.src.part, f32[1,3072]{1,0:T(1,128)S(1)} %halo1.13.part_h, f32[4,1024]{1,0:T(4,128)S(1)} %get-tuple-element.91.by_vel, ...), custom_call_target="tpu_custom_call" | custom-call | tf_op jit(solution)/shard_map/adjoint2/pallas_call | solution.py:373
  148.5 8.7 %halo4.4.grad_h = f32[4,3072]{1,0:T(4,128)S(1)} custom-call(f32[4,1024]{1,0:T(4,128)S(1)} %get-tuple-element.97.src.grad), custom_call_target="tpu_custom_call" | custom-call | tf_op jit(solution)/shard_map/halo4/pallas_call | solution.py:80
  161.9 6.8 %halo1.14.part_h = f32[1,3072]{1,0:T(1,128)S(1)} custom-call(f32[1,1024]{1,0:T(1,128)S(1)} %get-tuple-element.99.src.part), custom_call_target="tpu_custom_call" | custom-call | tf_op jit(solution)/shard_map/halo1/pallas_call | solution.py:80
  168.8 5.6 %adjoint2.6 = (f32[4,1024]{1,0:T(4,128)S(1)}, f32[8,1024]{1,0:T(8,128)S(1)}) custom-call(s32[1,128]{1,0:T(1,128)S(1)} %get-tuple-element.59.cnt, s32[32,128]{1,0:T(8,128)S(1)} %get-tuple-element.67.win, f32[1,1024]{1,0:T(1,128)S(1)} %get-tuple-element.99.src.part, f32[1,3072]{1,0:T(1,128)S(1)} %halo1.14.part_h, f32[4,1024]{1,0:T(4,128)S(1)} %get-tuple-element.100.by_vel, ...), custom_call_target="tpu_custom_call" | custom-call | tf_op jit(solution)/shard_map/adjoint2/pallas_call | solution.py:373
  174.4 8.8 %halo4.5.grad_h = f32[4,3072]{1,0:T(4,128)S(1)} custom-call(f32[4,1024]{1,0:T(4,128)S(1)} %get-tuple-element.106.src.grad), custom_call_target="tpu_custom_call" | custom-call | tf_op jit(solution)/shard_map/halo4/pallas_call | solution.py:80
  187.8 6.8 %halo1.15.part_h = f32[1,3072]{1,0:T(1,128)S(1)} custom-call(f32[1,1024]{1,0:T(1,128)S(1)} %get-tuple-element.108.src.part), custom_call_target="tpu_custom_call" | custom-call | tf_op jit(solution)/shard_map/halo1/pallas_call | solution.py:80
  194.6 6.0 %adjoint2.7 = (f32[4,1024]{1,0:T(4,128)}, f32[8,1024]{1,0:T(8,128)S(1)}) custom-call(s32[1,128]{1,0:T(1,128)S(1)} %get-tuple-element.59.cnt, s32[32,128]{1,0:T(8,128)S(1)} %get-tuple-element.62.win, f32[1,1024]{1,0:T(1,128)S(1)} %get-tuple-element.108.src.part, f32[1,3072]{1,0:T(1,128)S(1)} %halo1.15.part_h, f32[4,1024]{1,0:T(4,128)S(1)} %get-tuple-element.109.by_vel, ...), custom_call_target="tpu_custom_call" | custom-call | tf_op jit(solution)/shard_map/adjoint2/pallas_call | solution.py:373
  200.5 9.3 %collective-permute-start.3 = (f32[8,512]{1,0:T(8,128)S(1)}, f32[8,512]{1,0:T(8,128)S(1)}, u32[]{:S(2)}, u32[]{:S(2)}) collective-permute-start(f32[8,512]{1,0:T(8,128)S(1)} %get-tuple-element.127), channel_id=1, source_target_pairs={{32,0},{0,1},{33,2},{1,3},{34,4},{2,5},{35,6},{3,7},{6,8},{38,9},{... | collective-permute-start | bytes 49160 | tf_op jit(solution)/shard_map/ppermute | solution.py:653
  211.8 9.4 %collective-permute-done.2 = f32[8,512]{1,0:T(8,128)S(1)} collective-permute-done((f32[8,512]{1,0:T(8,128)S(1)}, f32[8,512]{1,0:T(8,128)S(1)}, u32[]{:S(2)}, u32[]{:S(2)}) %collective-permute-start.2) | collective-permute-done | bytes 16416 | tf_op jit(solution)/shard_map/ppermute | solution.py:652
  (43 shorter events, 55.8 us)
Async XLA Ops:
  4.4 14.0 %collective-permute-start.1 = (f32[16,512]{1,0:T(8,128)S(1)}, f32[16,512]{1,0:T(8,128)S(1)}, u32[]{:S(2)}, u32[]{:S(2)}) collective-permute-start(f32[16,512]{1,0:T(8,128)S(1)} %get-tuple-element.121), channel_id=1, source_target_pairs={{0,32},{1,0},{2,33},{3,1},{4,34},{5,2},{6,35},{7,3},{8,6},{9,38},{... | collective-permute-start | bytes 98312 | tf_op jit(solution)/shard_map/ppermute | solution.py:653
  14.2 6.8 %collective-permute-start = (f32[16,512]{1,0:T(8,128)S(1)}, f32[16,512]{1,0:T(8,128)S(1)}, u32[]{:S(2)}, u32[]{:S(2)}) collective-permute-start(f32[16,512]{1,0:T(8,128)S(1)} %get-tuple-element.122), channel_id=1, source_target_pairs={{0,0},{1,32},{2,1},{3,33},{4,2},{5,34},{6,3},{7,35},{8,38},{9,6},{... | collective-permute-start | bytes 98312 | tf_op jit(solution)/shard_map/ppermute | solution.py:652
  200.5 11.2 %collective-permute-start.3 = (f32[8,512]{1,0:T(8,128)S(1)}, f32[8,512]{1,0:T(8,128)S(1)}, u32[]{:S(2)}, u32[]{:S(2)}) collective-permute-start(f32[8,512]{1,0:T(8,128)S(1)} %get-tuple-element.127), channel_id=1, source_target_pairs={{32,0},{0,1},{33,2},{1,3},{34,4},{2,5},{35,6},{3,7},{6,8},{38,9},{... | collective-permute-start | bytes 49160 | tf_op jit(solution)/shard_map/ppermute | solution.py:653
  209.8 11.4 %collective-permute-start.2 = (f32[8,512]{1,0:T(8,128)S(1)}, f32[8,512]{1,0:T(8,128)S(1)}, u32[]{:S(2)}, u32[]{:S(2)}) collective-permute-start(f32[8,512]{1,0:T(8,128)S(1)} %get-tuple-element.128), channel_id=1, source_target_pairs={{0,0},{32,1},{1,2},{33,3},{2,4},{34,5},{3,6},{35,7},{38,8},{6,9},{... | collective-permute-start | bytes 49160 | tf_op jit(solution)/shard_map/ppermute | solution.py:652
